TPU v7x, 128 devices: a whole 4x4x4 slice. The times are simulated.
128 devices in a mesh: row: 16 (over y_lo, x, core), col: 8 (over y_hi, z).
Axes of the slice: x: 4, y: 4 (y_hi: 2, y_lo: 2; y = y_hi * 2 + y_lo), z: 4, core: 2. Of those that a mesh axis runs over, the one named last changes fastest.
Arguments:
- tokens: bfloat16 [2048, 8192], P('row', 'col'), may hold values from -6 to 6
- weights: bfloat16 [2, 14336, 8192], P(None, 'row', 'col'), may hold values from -0.0625 to 0.0625
- gradients: bfloat16 [2, 14336, 8192], P(None, 'row', 'col'), may hold values from -200 to 200, as said below
- row_factors: float32 [2, 14336], P(None, 'row'), may hold values from 0.05 to 0.5
- col_factors: float32 [2, 8192], P(None, 'col'), may hold values from 0.05 to 0.5
Outputs:
- hidden: bfloat16 [2048, 14336], P('col', 'row')
- row_new: float32 [2, 14336], P(None, 'row')
- col_new: float32 [2, 8192], P(None, 'col')
Inputs may be any that keep to these rules, and one draw needn't show every extreme that they name: Finite real gradients.
All inputs are finite; a program needn't handle non-finite values.
Results may differ from a plain program's by a relative error of at most 0.001.
The roundings to bfloat16 on the way count: a program that leaves them out, or rounds other values in their place, can miss the bound.
Values may be sent and summed in bfloat16 or wider, within the bound.
A program may use at most 128 MiB of HBM per device.

v0:
```python
import jax
import jax.numpy as jnp
from jax import lax
from jax.sharding import Mesh
from jax.sharding import PartitionSpec as P

D = 8192
FF = 14336
COL = ("col_0", "col_1")
ROW = ("row_0", "row_1", "row_2")
ROW_COL = ("row_0", "row_1", "row_2", "col_0", "col_1")


decay_rate = 0.5
learn_rate = 0.01
clip_limit = 1.0
tiny_eps = 1e-30


def copy_for_each(x, axis):
    copies = jnp.broadcast_to(x, (lax.axis_size(axis), *x.shape))
    return lax.all_to_all(copies, axis, split_axis=0, concat_axis=0, tiled=True)


def taken_together(x, axis):
    everything = copy_for_each(x, axis)
    return jnp.sum(everything, axis=0)


def by_axis(x, axes):
    for axis in axes:
        x = lax.psum(x, axis)
    return x


def local(tokens, weights, gradients, row_factors, col_factors):
    gradient = gradients.astype(jnp.float32)
    squares = gradient * gradient
    row_part = jnp.sum(squares, axis=2)
    col_part = jnp.sum(squares, axis=1)
    row_block = row_part.shape[1]
    col_block = col_part.shape[1]
    row_total = taken_together(row_part, COL)
    col_total = taken_together(col_part, ROW)
    row_new = decay_rate * row_factors + (1.0 - decay_rate) * (row_total / D + tiny_eps)
    col_new = decay_rate * col_factors + (1.0 - decay_rate) * (col_total / FF + tiny_eps)
    row_mean = taken_together(jnp.sum(row_new, axis=1), ROW) / FF
    denominator = jnp.sqrt(row_new[:, :, None] * col_new[:, None, :] / row_mean[:, None, None])
    update = gradient / denominator
    norm_total = by_axis(jnp.sum(update * update, axis=(1, 2)), ROW_COL)
    clip_scale = jnp.maximum(1.0, jnp.sqrt(norm_total / (FF * D)) / clip_limit)
    new_weights = (
        weights.astype(jnp.float32) - learn_rate * update / clip_scale[:, None, None]
    ).astype(jnp.bfloat16)
    spread = lax.all_gather(tokens, ROW, axis=0, tiled=True)
    flat_weights = new_weights.reshape(2 * row_block, col_block)
    combined = lax.psum_scatter(
        lax.dot_general(
            spread, flat_weights, (((1,), (1,)), ((), ())), preferred_element_type=jnp.float32
        ),
        COL,
        scatter_dimension=0,
        tiled=True,
    )
    gate_proj = combined[:, :row_block]
    up_proj = combined[:, row_block:]
    hidden = (jax.nn.silu(gate_proj) * up_proj).astype(jnp.bfloat16)
    return (hidden, row_new, col_new)


def solution(mesh):
    torus = Mesh(mesh.devices.reshape(2, 4, 2, 2, 4), ("row_0", "row_1", "row_2", "col_0", "col_1"))
    in_specs = (P(ROW, COL), P(None, ROW, COL), P(None, ROW, COL), P(None, ROW), P(None, COL))
    out_specs = (P(COL, ROW), P(None, ROW), P(None, COL))
    return jax.shard_map(local, mesh=torus, in_specs=in_specs, out_specs=out_specs, check_vma=False)
```

profile of v0, /device:TPU:1, one launch (start us, length us, event | category | flops | bytes accessed | tf_op | source)
XLA Modules:
  0.0 280.4 jit_solution(5089476382716384147)
XLA Ops:
  7.2 0.0 all-gather.2.cloned.1.call-start
  7.2 0.7 all-gather.2.cloned.1.call-update
  7.9 3.1 %fusion = (f32[2,1024]{1,0:T(2,128)S(1)}, f32[2,896]{1,0:T(2,128)S(1)}) fusion(bf16[2,896,1024]{2,1,0:T(8,128)(2,1)} %param.7), kind=kLoop, calls=%fused_computation.2 | loop fusion | flops 7336192 | bytes 3685376 | tf_op jit(solution)/shard_map/reduce_sum | solution.py:40
  11.0 15.0 %all_to_all.16 = f32[8,2,896]{2,1,0:T(2,128)S(1)} all-to-all(f32[8,2,896]{2,1,0:T(2,128)S(1)} %broadcast_in_dim.6), channel_id=1, replica_groups=mesh['row_0'=2,'row_1'=4,'row_2'=2,'col_0'=2,'col_1'=4] {'col_0','col_1'}, dimensions={0} | all-to-all | bytes 114688 | tf_op jit(solution)/shard_map/all_to_all | solution.py:22
  26.0 0.8 fusion.3
  26.8 11.8 %all_to_all.17 = f32[16,1,2]{2,1,0:T(1,128)S(1)} all-to-all(f32[16,1,2]{2,1,0:T(1,128)S(1)} %broadcast_in_dim.15), channel_id=1, replica_groups=mesh['row_0'=2,'row_1'=4,'row_2'=2,'col_0'=2,'col_1'=4] {'row_0','row_1'..., dimensions={0} | all-to-all | bytes 256 | tf_op jit(solution)/shard_map/all_to_all | solution.py:22
  38.7 0.7 broadcast_in_dim.14
  39.4 4.0 %all-to-all-start.1 = ((f32[16,2,1024]{2,1,0:T(2,128)}), f32[16,2,1024]{2,1,0:T(2,128)S(1)}, u32[]{:S(2)}, u32[]{:S(2)}) async-start(f32[16,2,1024]{2,1,0:T(2,128)} %broadcast_in_dim.14), calls=%async_computation.1 | async-start | bytes 262144 | tf_op jit(solution)/shard_map/all_to_all | solution.py:22
  43.3 0.0 reduce-scatter.2.cloned.1.call-start
  43.4 6.6 %all-to-all-done.1 = f32[16,2,1024]{2,1,0:T(2,128)S(1)} async-done(((f32[16,2,1024]{2,1,0:T(2,128)}), f32[16,2,1024]{2,1,0:T(2,128)S(1)}, u32[]{:S(2)}, u32[]{:S(2)}) %all-to-all-start.1) | async-done | bytes 131104 | tf_op jit(solution)/shard_map/all_to_all | solution.py:22
  50.1 0.1 reduce_sum.66
  50.1 0.7 add_multiply_fusion
  50.9 4.6 %multiply_reduce_fusion = f32[2]{0:T(128)S(1)} fusion(f32[2]{0:T(128)S(1)} %broadcast_multiply_fusion, f32[2,1024]{1,0:T(2,128)S(1)} %add_multiply_fusion, f32[2,896]{1,0:T(2,128)S(1)} %get-tuple-element.15, bf16[2,896,1024]{2,1,0:T(8,128)(2,1)} %param.7), kind=kLoop, calls=%fused_computation.6 | loop fusion | flops 11010046 | bytes 3685392 | tf_op jit(solution)/shard_map/reduce_sum | solution.py:50
  55.5 3.8 %psum.35 = f32[2]{0:T(128)S(1)} all-reduce(f32[2]{0:T(128)S(1)} %multiply_reduce_fusion), channel_id=1, replica_groups=mesh['row_0'=2,'row_1'=4,'row_2'=2,'col_0'=2,'col_1'=4] {'row_0'}, use_global_device_ids=true, to_apply=%region_7.0 | all-reduce | flops 2 | bytes 16 | tf_op jit(solution)/shard_map/psum | solution.py:32
  59.2 7.2 %psum.36 = f32[2]{0:T(128)S(1)} all-reduce(f32[2]{0:T(128)S(1)} %psum.35), channel_id=1, replica_groups=mesh['row_0'=2,'row_1'=4,'row_2'=2,'col_0'=2,'col_1'=4] {'row_1'}, use_global_device_ids=true, to_apply=%region_8.0 | all-reduce | flops 2 | bytes 16 | tf_op jit(solution)/shard_map/psum | solution.py:32
  66.4 5.4 %psum.37 = f32[2]{0:T(128)S(1)} all-reduce(f32[2]{0:T(128)S(1)} %psum.36), channel_id=1, replica_groups=mesh['row_0'=2,'row_1'=4,'row_2'=2,'col_0'=2,'col_1'=4] {'row_2'}, use_global_device_ids=true, to_apply=%region_9.0 | all-reduce | flops 2 | bytes 16 | tf_op jit(solution)/shard_map/psum | solution.py:32
  71.8 5.3 %psum.38 = f32[2]{0:T(128)S(1)} all-reduce(f32[2]{0:T(128)S(1)} %psum.37), channel_id=1, replica_groups=mesh['row_0'=2,'row_1'=4,'row_2'=2,'col_0'=2,'col_1'=4] {'col_0'}, use_global_device_ids=true, to_apply=%region_10.0 | all-reduce | flops 2 | bytes 16 | tf_op jit(solution)/shard_map/psum | solution.py:32
  77.1 6.6 %psum.39 = f32[2]{0:T(128)S(1)} all-reduce(f32[2]{0:T(128)S(1)} %psum.38), channel_id=1, replica_groups=mesh['row_0'=2,'row_1'=4,'row_2'=2,'col_0'=2,'col_1'=4] {'col_1'}, use_global_device_ids=true, to_apply=%region_11.0 | all-reduce | flops 2 | bytes 16 | tf_op jit(solution)/shard_map/psum | solution.py:32
  83.7 5.7 %subtract_convert_fusion = bf16[2,896,1024]{2,1,0:T(8,128)(2,1)} fusion(bf16[2,896,1024]{2,1,0:T(8,128)(2,1)} %param.6, f32[2]{0:T(128)S(1)} %sqrt_maximum_fusion, f32[2]{0:T(128)S(1)} %broadcast_multiply_fusion, f32[2,1024]{1,0:T(2,128)S(1)} %add_multiply_fusion, f32[2,896]{1,0:T(2,128)S(1)} %get-tuple-element.15, bf16[2,896,1024]{2,1,0:T(8,128)(2,1)} %param.7), kind=kLoop, calls=%fused_computation.5 | loop fusion | flops 16515072 | bytes 11025424 | tf_op jit(solution)/shard_map/convert_element_type | solution.py:54
  89.4 0.0 all-gather.2.cloned.1.call-done
  89.4 13.8 %convolution_bitcast_fusion = f32[2048,1792]{0,1:T(8,128)} fusion(bf16[1792,1024]{1,0:T(8,128)(2,1)} %bitcast.5, bf16[2048,1024]{1,0:T(8,128)(2,1)} %all-gather.2.cloned.1.call-done), kind=kOutput, calls=%fused_computation.4 | convolution fusion | flops 7516192768 | bytes 22544384 | tf_op jit(solution)/shard_map/dot_general | solution.py:58
  103.2 167.6 %reduce-scatter.2.cloned.1.call-done = f32[256,1792]{0,1:T(8,128)} async-done(((f32[2048,1792]{0,1:T(8,128)}), f32[256,1792]{0,1:T(8,128)}) %reduce-scatter.2.cloned.1.call-update) | async-done | bytes 1835024 | tf_op jit(solution)/shard_map/reduce_scatter | solution.py:57
  270.9 1.7 fusion.2
  272.6 1.0 copy.13
  (11 shorter events, 0.1 us)
Async XLA Ops:
  7.2 82.3 %all-gather.2.cloned.1.call-start = ((), (), s32[]{:S(2)}) async-start(), calls=%async_computation.4 | async-start | bytes 4456448 | tf_op jit(solution)/shard_map/all_gather | solution.py:55
  26.8 62.6 %copy-start.1 = (f32[2,896]{1,0:T(2,128)}, f32[2,896]{1,0:T(2,128)S(1)}, u32[]{:S(2)}) copy-start(f32[2,896]{1,0:T(2,128)S(1)} %get-tuple-element.15) | copy-start | bytes 21508
  39.4 10.7 %all-to-all-start.1 = ((f32[16,2,1024]{2,1,0:T(2,128)}), f32[16,2,1024]{2,1,0:T(2,128)S(1)}, u32[]{:S(2)}, u32[]{:S(2)}) async-start(f32[16,2,1024]{2,1,0:T(2,128)} %broadcast_in_dim.14), calls=%async_computation.1 | async-start | bytes 262144 | tf_op jit(solution)/shard_map/all_to_all | solution.py:22
  43.3 227.5 %reduce-scatter.2.cloned.1.call-start = ((), (), s32[]{:S(2)}) async-start(), calls=%async_computation.5 | async-start | bytes 16515072 | tf_op jit(solution)/shard_map/reduce_scatter | solution.py:57
  50.8 38.6 %copy-start = (f32[2,1024]{1,0:T(2,128)}, f32[2,1024]{1,0:T(2,128)S(1)}, u32[]{:S(2)}) copy-start(f32[2,1024]{1,0:T(2,128)S(1)} %add_multiply_fusion) | copy-start | bytes 24580
Sparse Core Ops, SparseCore 0:
  9.7 40.9 all-gather.1
  103.4 167.4 reduce-scatter.1
where the time goes:
time: 281 us; the launch traced here: 280 us
  waiting for transfers between devices  175 us (62%)
  blocking collectives  55 us (20%)
  other arithmetic  16.8 us (6%)
  between operations  14.1 us (5%)
  matrix products  13.8 us (5%)
  starting transfers between devices  4.04 us (1%)
    reduce_scatter x1, waiting for transfers between devices, local(): lax.psum_scatter(lax.dot_general(spread, flat_weights, (((1,), (1,)), (()...  168 us
    psum x5, blocking collectives, by_axis(): x = lax.psum(x, axis)  28.2 us
    all_to_all x2, blocking collectives, copy_for_each(): return lax.all_to_all(copies, axis, split_axis=0, concat_axis=0, tiled=True)  26.8 us
    dot_general x1, matrix products, local(): lax.dot_general(spread, flat_weights, (((1,), (1,)), ((), ())), preferred...  13.8 us
    all_to_all x1, waiting for transfers between devices, copy_for_each(): return lax.all_to_all(copies, axis, split_axis=0, concat_axis=0, tiled=True)  6.65 us
    convert_element_type x1, other arithmetic, local(): new_weights = (weights.astype(jnp.float32) - learn_rate * update / clip_s...  5.73 us
  transfers between devices with their start and end apart: 3, of which 2 were waited for; matrix products, arithmetic and copies ran while one was open for 6% of the time, Pallas kernels for 0%

commit v1 on v0

v1 whole, which is shorter than its diff:
```python
import jax
import jax.numpy as jnp
from jax import lax
from jax.experimental import pallas as pl
from jax.experimental.pallas import tpu as pltpu
from jax.sharding import Mesh
from jax.sharding import PartitionSpec as P

D = 8192
FF = 14336
AXES = ("yl", "x", "c", "yh", "z")
ROW = ("yl", "x", "c")
COL = ("yh", "z")
F32 = jnp.float32
BF16 = jnp.bfloat16
BY_MESH = pl.DeviceIdType.MESH

decay_rate = 0.5
learn_rate = 0.01
clip_limit = 1.0
tiny_eps = 1e-30

ROWS = 896
COLS = 1024
UNIT = 128
CHUNKS = ROWS // UNIT
LANES = 128
TILES = COLS // LANES
HALF = 1024
BLOCK = 256

COL_YL, ROW_YH, COL_C, ROW_Z, COL_X, SUM_C, SUM_X, SUM_Z, SUM_Y = 0, 1, 2, 3, 7, 11, 12, 16, 20
STAT_SEMS = 24


def spread(row):
    return jnp.transpose(jnp.broadcast_to(row, (LANES, LANES)))


def kernel(
    tok, wgt, grd, rowf, colf,
    out, row_out, col_out,
    g, w, wown, wpart, t, p, r, hid,
    colacc, colsrc, rowsrc, col_yl, row_yh, col_c, row_z, col_x,
    rn, cn, a, b, sumsrc, sum_c, sum_x, sum_z, sum_y,
    g_sem, w_sem, st_s, st_r, ty_s, ty_r, tx_s, tx_r, tc_s, tc_r, self_sem,
    wy_s, wy_r, rs_s, rs_r, out_sem,
):
    yl = lax.axis_index("yl")
    x = lax.axis_index("x")
    c = lax.axis_index("c")
    yh = lax.axis_index("yh")
    z = lax.axis_index("z")
    y = 2 * yh + yl

    def at_y(q):
        return {"yh": lax.div(q, 2), "yl": lax.rem(q, 2)}

    others = [1, 2, 3]
    x_of = [lax.rem(x + d, 4) for d in others]
    y_of = [lax.rem(y + d, 4) for d in others]
    z_of = [lax.rem(z + d, 4) for d in others]
    sibling = {"c": 1 - c}
    yl_peer = {"yl": 1 - yl}
    yh_peer = {"yh": 1 - yh}

    def remote(src, dst, s, q, device):
        return pltpu.make_async_remote_copy(
            src_ref=src, dst_ref=dst, send_sem=s, recv_sem=q,
            device_id=device, device_id_type=BY_MESH,
        )

    def g_copy(m, k):
        rows = pl.ds(k * UNIT, UNIT)
        return pltpu.make_async_copy(grd.at[m, rows], g.at[m, rows], g_sem.at[m, k])

    for m in range(2):
        for k in range(CHUNKS):
            g_copy(m, k).start()
    w_copies = [pltpu.make_async_copy(wgt.at[m], w.at[m], w_sem.at[m]) for m in range(2)]
    for copy in w_copies:
        copy.start()

    barrier = pltpu.get_barrier_semaphore()
    peers = [sibling]
    peers += [{"x": q} for q in x_of] + [at_y(q) for q in y_of] + [{"z": q} for q in z_of]
    for device in peers:
        pl.semaphore_signal(barrier, inc=1, device_id=device, device_id_type=BY_MESH)
    pl.semaphore_wait(barrier, len(peers))

    colacc[...] = jnp.zeros_like(colacc)
    rn[...] = jnp.ones_like(rn)
    rowsrc[...] = jnp.zeros_like(rowsrc)
    for m in range(2):
        def squares(k, carry):
            g_copy(m, k).wait()
            rows = pl.ds(pl.multiple_of(k * UNIT, UNIT), UNIT)
            total = jnp.zeros((UNIT, LANES), F32)
            for j in range(TILES):
                v = g[m, rows, j * LANES:(j + 1) * LANES].astype(F32)
                v = v * v
                total = total + v
                colacc[m * TILES + j] += jnp.sum(v.reshape(UNIT // 8, 8, LANES), axis=0)
            rowsrc[0, pl.ds(m * CHUNKS + k, 1), :] = jnp.sum(
                jnp.transpose(total), axis=0, keepdims=True
            )
            return carry

        lax.fori_loop(0, CHUNKS, squares, 0)
    colsrc[0] = jnp.sum(colacc[...], axis=1)

    to_yl = remote(colsrc.at[0], col_yl, st_s.at[COL_YL], st_r.at[COL_YL], yl_peer)
    to_yh = remote(rowsrc.at[0], row_yh, st_s.at[ROW_YH], st_r.at[ROW_YH], yh_peer)
    to_yl.start()
    to_yh.start()
    to_yl.wait_recv()
    colsrc[1] = colsrc[0] + col_yl[...]
    to_c = remote(colsrc.at[1], col_c, st_s.at[COL_C], st_r.at[COL_C], sibling)
    to_c.start()
    to_yh.wait_recv()
    rowsrc[1] = rowsrc[0] + row_yh[...]
    row_sends = []
    for q in z_of:
        copy = remote(rowsrc.at[1], row_z.at[z], st_s.at[ROW_Z + q], st_r.at[ROW_Z + z], {"z": q})
        copy.start()
        row_sends.append(copy)
    row_z[z] = rowsrc[1]

    home = (x * 2 + c) * 128
    mine = pl.ds(pl.multiple_of(home, 128), 128)

    def token_send(q):
        return remote(tok, t.at[yh, mine], ty_s.at[q], ty_r.at[yh], {"yh": yl, "yl": q})

    self_copy = pltpu.make_async_copy(tok, t.at[yh, mine], self_sem)
    for q in range(2):
        stays = (yl == q) & (yh == q)

        @pl.when(jnp.logical_not(stays))
        def _():
            token_send(q).start()

        @pl.when(stays)
        def _():
            self_copy.start()

    to_c.wait_recv()
    colsrc[2] = colsrc[1] + col_c[...]
    col_sends = []
    for q in x_of:
        copy = remote(colsrc.at[2], col_x.at[x], st_s.at[COL_X + q], st_r.at[COL_X + x], {"x": q})
        copy.start()
        col_sends.append(copy)
    col_x[x] = colsrc[2]

    for q in z_of:
        remote(rowsrc.at[1], row_z.at[q], st_s.at[ROW_Z + q], st_r.at[ROW_Z + q], {"z": q}).wait_recv()
    row_total = ((row_z[0] + row_z[1]) + row_z[2]) + row_z[3]
    for m in range(2):
        for k in range(CHUNKS):
            i = m * CHUNKS + k
            rn[i:i + 1] = decay_rate * rowf[m:m + 1, k * UNIT:(k + 1) * UNIT] + (1.0 - decay_rate) * (
                row_total[i:i + 1] / D + tiny_eps
            )
            row_out[m:m + 1, k * UNIT:(k + 1) * UNIT] = rn[i:i + 1]
    for q in x_of:
        remote(colsrc.at[2], col_x.at[q], st_s.at[COL_X + q], st_r.at[COL_X + q], {"x": q}).wait_recv()
    col_total = ((col_x[0] + col_x[1]) + col_x[2]) + col_x[3]
    for m in range(2):
        for j in range(TILES):
            i = m * TILES + j
            cn[i:i + 1] = decay_rate * colf[m:m + 1, j * LANES:(j + 1) * LANES] + (1.0 - decay_rate) * (
                col_total[i:i + 1] / FF + tiny_eps
            )
            col_out[m:m + 1, j * LANES:(j + 1) * LANES] = cn[i:i + 1]

    a[...] = 1.0 / rn[...]
    b[...] = 1.0 / cn[...]
    sumsrc[...] = jnp.zeros_like(sumsrc)
    for m in range(2):
        def norms(k, carry):
            rows = pl.ds(pl.multiple_of(k * UNIT, UNIT), UNIT)
            total = jnp.zeros((UNIT, LANES), F32)
            for j in range(TILES):
                v = g[m, rows, j * LANES:(j + 1) * LANES].astype(F32)
                total = total + v * v * b[m * TILES + j:m * TILES + j + 1]
            total = total * spread(a[pl.ds(m * CHUNKS + k, 1), :])
            return carry + jnp.sum(total.reshape(UNIT // 8, 8, LANES), axis=0)

        parts = lax.fori_loop(0, CHUNKS, norms, jnp.zeros((8, LANES), F32))
        sumsrc[0, m:m + 1] = jnp.sum(parts, axis=0, keepdims=True)
        sumsrc[0, 2 + m:3 + m] = jnp.sum(rn[m * CHUNKS:(m + 1) * CHUNKS], axis=0, keepdims=True)

    sum_sends = []
    to_c2 = remote(sumsrc.at[0], sum_c, st_s.at[SUM_C], st_r.at[SUM_C], sibling)
    to_c2.start()
    to_c2.wait_recv()
    sumsrc[1] = sumsrc[0] + sum_c[...]

    def exchange(src, dst, place, me, peers_of, device):
        for q in peers_of:
            copy = remote(src, dst.at[me], st_s.at[place + q], st_r.at[place + me], device(q))
            copy.start()
            sum_sends.append(copy)
        dst[me] = src[...]
        for q in peers_of:
            remote(src, dst.at[q], st_s.at[place + q], st_r.at[place + q], device(q)).wait_recv()
        return ((dst[0] + dst[1]) + dst[2]) + dst[3]

    sumsrc[2] = exchange(sumsrc.at[1], sum_x, SUM_X, x, x_of, lambda q: {"x": q})

    for q in range(2):
        stays = (yl == yh) & (yh == q)

        @pl.when(jnp.logical_not(stays))
        def _():
            remote(tok, t.at[q, mine], ty_s.at[q], ty_r.at[q], {"yh": yl, "yl": q}).wait_recv()

        @pl.when(stays)
        def _():
            self_copy.wait()

    def rows_of(q, core):
        return pl.ds(pl.multiple_of((q * 2 + core) * 128, 128), 128)

    def along_x(q, f, source):
        rows = rows_of(source, c)
        return remote(t.at[f, rows], t.at[f, rows], tx_s.at[q, f], tx_r.at[source, f], {"x": q})

    def to_sibling(q, f):
        rows = rows_of(q, c)
        return remote(t.at[f, rows], t.at[f, rows], tc_s.at[q, f], tc_r.at[q, f], sibling)

    for q in [x_of[0], x_of[2], x_of[1]]:
        for f in range(2):
            along_x(q, f, x).start()
    for f in range(2):
        to_sibling(x, f).start()

    sumsrc[3] = exchange(sumsrc.at[2], sum_z, SUM_Z, z, z_of, lambda q: {"z": q})
    total = exchange(sumsrc.at[3], sum_y, SUM_Y, y, y_of, at_y)

    for m in range(2):
        row_mean = jnp.sum(total[2 + m:3 + m], axis=1, keepdims=True) / (8.0 * FF)
        norm_total = jnp.sum(total[m:m + 1], axis=1, keepdims=True) * row_mean
        clip_scale = jnp.maximum(1.0, jnp.sqrt(norm_total / (FF * D)) / clip_limit)
        scale = learn_rate * jnp.sqrt(row_mean) / clip_scale
        a[m * CHUNKS:(m + 1) * CHUNKS] = scale / jnp.sqrt(rn[m * CHUNKS:(m + 1) * CHUNKS])
    b[...] = 1.0 / jnp.sqrt(cn[...])

    for copy in w_copies:
        copy.wait()

    def weight_send(k):
        return remote(wown.at[k], wpart.at[k], wy_s.at[k], wy_r.at[k], yh_peer)

    def update(k, carry):
        rows = pl.ds(pl.multiple_of(k * UNIT, UNIT), UNIT)
        for m in range(2):
            factor = spread(a[pl.ds(m * CHUNKS + k, 1), :])
            for j in range(TILES):
                cols = slice(j * LANES, (j + 1) * LANES)
                step = g[m, rows, cols].astype(F32) * factor * b[m * TILES + j:m * TILES + j + 1]
                wown[k, m * UNIT:(m + 1) * UNIT, cols] = (w[m, rows, cols].astype(F32) - step).astype(BF16)
        weight_send(k).start()
        return carry

    lax.fori_loop(0, CHUNKS, update, 0)

    for q in [x_of[0], x_of[2], x_of[1]]:
        for f in range(2):
            along_x(q, f, q).wait_recv()
            to_sibling(q, f).start()
    for q in [x] + [x_of[0], x_of[2], x_of[1]]:
        for f in range(2):
            rows = rows_of(q, 1 - c)
            remote(t.at[f, rows], t.at[f, rows], tc_s.at[q, f], tc_r.at[q, f], sibling).wait_recv()

    right = lax.rem(z + 1, 4)
    left = lax.rem(z + 3, 4)

    def block_of(side, s):
        return lax.rem(z + 3 - s, 4) if side == 0 else lax.rem(z + 1 + s, 4)

    def ring_copy(k, s, side):
        target = right if side == 0 else left
        return remote(
            p.at[k, block_of(side, s), side], r.at[k, s, side],
            rs_s.at[k, s, side], rs_r.at[k, s, side], {"z": target},
        )

    def times(i, k, half, weights):
        tokens = t[half, pl.ds(pl.multiple_of(i * BLOCK, BLOCK), BLOCK), :]
        return lax.dot_general(
            tokens, weights[k], (((1,), (1,)), ((), ())), preferred_element_type=F32
        )

    def own_products(k):
        def body(i, carry):
            v = times(i, k, yh, wown)
            p[k, i, 0] = v[:, :UNIT]
            p[k, i, 1] = v[:, UNIT:]
            return carry

        lax.fori_loop(0, 4, body, 0)

    def other_products(k):
        def body(i, carry):
            v = times(i, k, 1 - yh, wpart)
            p[k, i, 0] += v[:, :UNIT]
            p[k, i, 1] += v[:, UNIT:]
            return carry

        lax.fori_loop(0, 4, body, 0)

    def ring_step(k, s):
        for side in range(2):
            ring_copy(k, s - 1, side).wait_recv()
            p[k, block_of(side, s), side] += r[k, s - 1, side]
            ring_copy(k, s, side).start()

    def out_copy(k):
        return pltpu.make_async_copy(
            hid.at[k], out.at[:, pl.ds(pl.multiple_of(k * UNIT, UNIT), UNIT)], out_sem.at[k]
        )

    def finish(k):
        for side in range(2):
            ring_copy(k, 2, side).wait_recv()
        gate = p[k, z, 0] + r[k, 2, 0]
        up = p[k, z, 1] + r[k, 2, 1]
        hid[k] = (gate / (1.0 + jnp.exp(-gate)) * up).astype(BF16)
        out_copy(k).start()

    def work(i, carry):
        @pl.when(i < CHUNKS)
        def _():
            own_products(i)

        @pl.when((i >= 1) & (i < CHUNKS + 1))
        def _():
            ring_step(i - 1, 1)

        @pl.when((i >= 2) & (i < CHUNKS + 2))
        def _():
            ring_step(i - 2, 2)

        @pl.when(i >= 3)
        def _():
            finish(i - 3)

        @pl.when(i < CHUNKS)
        def _():
            weight_send(i).wait_recv()
            other_products(i)
            for side in range(2):
                ring_copy(i, 0, side).start()

        return carry

    lax.fori_loop(0, CHUNKS + 3, work, 0)

    to_yl.wait_send()
    to_yh.wait_send()
    to_c.wait_send()
    to_c2.wait_send()
    for copy in row_sends + col_sends + sum_sends:
        copy.wait_send()
    for q in range(2):
        @pl.when(jnp.logical_not((yl == q) & (yh == q)))
        def _():
            token_send(q).wait_send()
    for q in x_of:
        for f in range(2):
            along_x(q, f, x).wait_send()
    for q in range(4):
        for f in range(2):
            to_sibling(q, f).wait_send()

    def drain(k, carry):
        weight_send(k).wait_send()
        for s in range(3):
            for side in range(2):
                ring_copy(k, s, side).wait_send()
        out_copy(k).wait()
        return carry

    lax.fori_loop(0, CHUNKS, drain, 0)


def local(tokens, weights, gradients, row_factors, col_factors):
    vmem = pl.BlockSpec(memory_space=pltpu.VMEM)
    hbm = pl.BlockSpec(memory_space=pl.ANY)
    dma = pltpu.SemaphoreType.DMA
    scratch = [
        pltpu.VMEM((2, ROWS, COLS), BF16),
        pltpu.VMEM((2, ROWS, COLS), BF16),
        pltpu.VMEM((CHUNKS, 2 * UNIT, COLS), BF16),
        pltpu.VMEM((CHUNKS, 2 * UNIT, COLS), BF16),
        pltpu.VMEM((2, HALF, COLS), BF16),
        pltpu.VMEM((CHUNKS, 4, 2, BLOCK, UNIT), F32),
        pltpu.VMEM((CHUNKS, 3, 2, BLOCK, UNIT), F32),
        pltpu.VMEM((CHUNKS, BLOCK, UNIT), BF16),
        pltpu.VMEM((16, 8, LANES), F32),
        pltpu.VMEM((3, 16, LANES), F32),
        pltpu.VMEM((2, 16, LANES), F32),
        pltpu.VMEM((16, LANES), F32),
        pltpu.VMEM((16, LANES), F32),
        pltpu.VMEM((16, LANES), F32),
        pltpu.VMEM((4, 16, LANES), F32),
        pltpu.VMEM((4, 16, LANES), F32),
        pltpu.VMEM((16, LANES), F32),
        pltpu.VMEM((16, LANES), F32),
        pltpu.VMEM((16, LANES), F32),
        pltpu.VMEM((16, LANES), F32),
        pltpu.VMEM((4, 8, LANES), F32),
        pltpu.VMEM((8, LANES), F32),
        pltpu.VMEM((4, 8, LANES), F32),
        pltpu.VMEM((4, 8, LANES), F32),
        pltpu.VMEM((4, 8, LANES), F32),
        dma((2, CHUNKS)), dma((2,)), dma((STAT_SEMS,)), dma((STAT_SEMS,)),
        dma((2,)), dma((2,)), dma((4, 2)), dma((4, 2)), dma((4, 2)), dma((4, 2)), dma(()),
        dma((CHUNKS,)), dma((CHUNKS,)), dma((CHUNKS, 3, 2)), dma((CHUNKS, 3, 2)), dma((CHUNKS,)),
    ]
    return pl.pallas_call(
        kernel,
        out_shape=[
            jax.ShapeDtypeStruct((BLOCK, ROWS), BF16),
            jax.ShapeDtypeStruct((2, ROWS), F32),
            jax.ShapeDtypeStruct((2, COLS), F32),
        ],
        in_specs=[hbm, hbm, hbm, vmem, vmem],
        out_specs=[hbm, vmem, vmem],
        scratch_shapes=scratch,
        compiler_params=pltpu.CompilerParams(
            collective_id=0, has_side_effects=True, vmem_limit_bytes=60 * 2**20
        ),
        name="step",
    )(tokens, weights, gradients, row_factors, col_factors)


def solution(mesh):
    torus = Mesh(mesh.devices.reshape(2, 4, 2, 2, 4), AXES)
    in_specs = (P(ROW, COL), P(None, ROW, COL), P(None, ROW, COL), P(None, ROW), P(None, COL))
    out_specs = (P(COL, ROW), P(None, ROW), P(None, COL))
    return jax.shard_map(local, mesh=torus, in_specs=in_specs, out_specs=out_specs, check_vma=False)
```

time: 281 us -> 133 us (0.47)
  waiting for transfers between devices: 175 us -> 0 us
  Pallas kernels: 0 us -> 126 us
  blocking collectives: 55 us -> 0 us
  other arithmetic: 16.8 us -> 0 us
  matrix products: 13.8 us -> 0 us
  between operations: 14.1 us -> 0.64 us
  starting transfers between devices: 4.04 us -> 0 us
    reduce_scatter x1 -> x0, waiting for transfers between devices: 168 us -> none  [local(): lax.psum_scatter(lax.dot_general(spread, flat_weights, (((1,), (1,)), (()...]
    pallas_call x0 -> x1, Pallas kernels: none -> 126 us  [local(): pl.pallas_call(kernel, out_shape=[jax.ShapeDtypeStruct((BLOCK, ROWS), BF1...]
    psum x5 -> x0, blocking collectives: 28.2 us -> none  [by_axis(): x = lax.psum(x, axis)]
    all_to_all x2 -> x0, blocking collectives: 26.8 us -> none  [copy_for_each(): return lax.all_to_all(copies, axis, split_axis=0, concat_axis=0, tiled=True)]
    dot_general x1 -> x0, matrix products: 13.8 us -> none  [local(): lax.dot_general(spread, flat_weights, (((1,), (1,)), ((), ())), preferred...]
    reduce_sum x6 -> x0, other arithmetic: 8.65 us -> none  [the longest x1 4.62 us: local(): norm_total = by_axis(jnp.sum(update * update, axis=(1, 2)), ROW_COL)]
    convert_element_type x2 -> x0, other arithmetic: 7.45 us -> none  [the longest x1 5.73 us: local(): new_weights = (weights.astype(jnp.float32) - learn_rate * update / clip_s...]
    all_to_all x1 -> x0, waiting for transfers between devices: 6.65 us -> none  [copy_for_each(): return lax.all_to_all(copies, axis, split_axis=0, concat_axis=0, tiled=True)]
  transfers between devices with their start and end apart: 3 -> 0, of which waited for: 2 -> 0; matrix products, arithmetic and copies ran while one was open for 6% -> 0% of each run, Pallas kernels for 0% -> 0%
where the time goes in v1:
time: 133 us; the launch traced here: 131 us
  Pallas kernels  126 us (95%)
  local copies, waits for them, and re-layouts  4.41 us (3%)
    pallas_call x1, Pallas kernels, local(): pl.pallas_call(kernel, out_shape=[jax.ShapeDtypeStruct((BLOCK, ROWS), BF1...  126 us
    unnamed x3, local copies, waits for them, and re-layouts  4.41 us

profile of v1, /device:TPU:1, one launch (start us, length us, event | category | flops | bytes accessed | tf_op | source)
XLA Modules:
  0.0 131.3 jit_solution(13167978216651464544)
XLA Ops:
  0.6 126.3 %step.1 = (bf16[256,896]{1,0:T(8,128)(2,1)}, f32[2,896]{1,0:T(2,128)}, f32[2,1024]{1,0:T(2,128)}) custom-call(bf16[128,1024]{1,0:T(8,128)(2,1)} %tok.1, bf16[2,896,1024]{2,1,0:T(8,128)(2,1)} %wgt.1, bf16[2,896,1024]{2,1,0:T(8,128)(2,1)} %grd.1, f32[2,896]{1,0:T(2,128)} %rowf.1, f32[2,1024]{1,0:T(2,128)} %colf.1), custom_call_target="tpu_custom_call" | custom-call | tf_op jit(solution)/shard_map/step/pallas_call | solution.py:425
  126.9 1.8 %copy.11 = bf16[256,896]{1,0:T(8,128)(2,1)} copy(bf16[256,896]{1,0:T(8,128)(2,1)} %get-tuple-element.6) | data formatting | bytes 917504
  128.8 1.3 copy.12
  130.0 1.3 copy.13

commit v2 on v1

v2 whole, which is shorter than its diff:
```python
import jax
import jax.numpy as jnp
from jax import lax
from jax.experimental import pallas as pl
from jax.experimental.pallas import tpu as pltpu
from jax.sharding import Mesh
from jax.sharding import PartitionSpec as P

D = 8192
FF = 14336
AXES = ("yl", "x", "c", "yh", "z")
ROW = ("yl", "x", "c")
COL = ("yh", "z")
F32 = jnp.float32
BF16 = jnp.bfloat16
BY_MESH = pl.DeviceIdType.MESH

decay_rate = 0.5
learn_rate = 0.01
clip_limit = 1.0
tiny_eps = 1e-30

ROWS = 896
COLS = 1024
UNIT = 128
PAIRS = ROWS // UNIT
PIECE = 64
CHUNKS = ROWS // PIECE
LOCAL = 2
RINGS = CHUNKS + LOCAL
LAG = 2
LANES = 128
TILES = COLS // LANES
HALF = 1024
BLOCK = 256

COL_SUMS, ROW_SUMS, SUM_XC, SUM_YZ = 0, 16, 24, 32
STAT_SEMS = 48


def spread(row):
    return jnp.transpose(jnp.broadcast_to(row, (LANES, LANES)))


def kernel(
    tok, wgt, grd, rowf, colf,
    hid, row_out, col_out,
    g, w, wown, wpart, t, p, r, away, come, kept,
    colacc, colsrc, rowsrc, colin, rowin,
    rn, cn, a, b, sumsrc, sum_xc, sum_yz,
    g_sem, w_sem, st_s, st_r, ty_s, ty_r, tx_s, tx_r, tc_s, tc_r,
    wy_s, wy_r, rs_s, rs_r, fy_s, fy_r,
):
    yl = lax.axis_index("yl")
    x = lax.axis_index("x")
    c = lax.axis_index("c")
    yh = lax.axis_index("yh")
    z = lax.axis_index("z")
    y = 2 * yh + yl

    def at_row(q):
        return {"yl": lax.div(q, 8), "x": lax.rem(lax.div(q, 2), 4), "c": lax.rem(q, 2)}

    def at_col(q):
        return {"yh": lax.div(q, 4), "z": lax.rem(q, 4)}

    def at_xc(q):
        return {"x": lax.div(q, 2), "c": lax.rem(q, 2)}

    def at_yz(q):
        return {"yh": lax.div(q, 8), "yl": lax.rem(lax.div(q, 4), 2), "z": lax.rem(q, 4)}

    in_row = yl * 8 + x * 2 + c
    in_col = yh * 4 + z
    in_xc = x * 2 + c
    in_yz = y * 4 + z
    x_of = [lax.rem(x + d, 4) for d in (1, 3, 2)]
    sibling = {"c": 1 - c}
    yh_peer = {"yh": 1 - yh}

    def remote(src, dst, s, q, device):
        return pltpu.make_async_remote_copy(
            src_ref=src, dst_ref=dst, send_sem=s, recv_sem=q,
            device_id=device, device_id_type=BY_MESH,
        )

    def g_copy(m, k):
        rows = pl.ds(k * UNIT, UNIT)
        return pltpu.make_async_copy(grd.at[m, rows], g.at[m, rows], g_sem.at[m, k])

    for m in range(2):
        for k in range(PAIRS):
            g_copy(m, k).start()
    w_copies = [pltpu.make_async_copy(wgt.at[m], w.at[m], w_sem.at[m]) for m in range(2)]
    for copy in w_copies:
        copy.start()

    barrier = pltpu.get_barrier_semaphore()
    peers = [at_row(lax.rem(in_row + d, 16)) for d in range(1, 16)]
    peers += [at_yz(lax.rem(in_yz + d, 16)) for d in range(1, 16)]
    for device in peers:
        pl.semaphore_signal(barrier, inc=1, device_id=device, device_id_type=BY_MESH)
    colacc[...] = jnp.zeros_like(colacc)
    rn[...] = jnp.ones_like(rn)
    rowsrc[...] = jnp.zeros_like(rowsrc)
    for m in range(2):
        def squares(k, carry):
            g_copy(m, k).wait()
            rows = pl.ds(pl.multiple_of(k * UNIT, UNIT), UNIT)
            total = jnp.zeros((UNIT, LANES), F32)
            for j in range(TILES):
                v = g[m, rows, j * LANES:(j + 1) * LANES].astype(F32)
                v = v * v
                total = total + v
                colacc[m * TILES + j] += jnp.sum(v.reshape(UNIT // 8, 8, LANES), axis=0)
            rowsrc[pl.ds(m * PAIRS + k, 1), :] = jnp.sum(
                jnp.transpose(total), axis=0, keepdims=True
            )
            return carry

        lax.fori_loop(0, PAIRS, squares, 0)
    colsrc[...] = jnp.sum(colacc[...], axis=1)
    pl.semaphore_wait(barrier, len(peers))

    sent = []

    def give(src, slots, place, n, me, device_of):
        for d in range(1, n):
            q = lax.rem(me + d, n)
            copy = remote(src, slots.at[me], st_s.at[place + q], st_r.at[place + me], device_of(q))
            copy.start()
            sent.append(copy)
        slots[me] = src[...]

    def take(src, slots, place, n, me, device_of):
        for d in range(1, n):
            q = lax.rem(me + d, n)
            remote(src, slots.at[q], st_s.at[place + q], st_r.at[place + q], device_of(q)).wait_recv()
        total = slots[0]
        for q in range(1, n):
            total = total + slots[q]
        return total

    give(rowsrc, rowin, ROW_SUMS, 8, in_col, at_col)
    give(colsrc, colin, COL_SUMS, 16, in_row, at_row)

    def rows_of(q, core):
        return pl.ds(pl.multiple_of((q * 2 + core) * 128, 128), 128)

    mine = rows_of(x, c)
    same = yl == yh

    def token_send(q):
        return remote(tok, t.at[yh, mine], ty_s.at[q], ty_r.at[yh], {"yh": yl, "yl": q})

    other_send = remote(tok, t.at[2, mine], ty_s.at[2], ty_r.at[2], {"yl": 1 - yl})
    home = jnp.where(same, yh, 2)
    t[home, mine] = tok[...]
    early = [
        remote(tok, t.at[home, mine], tx_s.at[q, jnp.where(same, 0, 1)], tx_r.at[x, jnp.where(same, 0, 1)], {"x": q})
        for q in x_of[:2]
    ]
    for copy in early:
        copy.start()
    for q in range(2):
        @pl.when(jnp.logical_not(same & (yh == q)))
        def _():
            token_send(q).start()

    @pl.when(jnp.logical_not(same))
    def _():
        other_send.start()

    row_total = take(rowsrc, rowin, ROW_SUMS, 8, in_col, at_col)
    for m in range(2):
        for k in range(PAIRS):
            i = m * PAIRS + k
            rn[i:i + 1] = decay_rate * rowf[m:m + 1, k * UNIT:(k + 1) * UNIT] + (1.0 - decay_rate) * (
                row_total[i:i + 1] / D + tiny_eps
            )
            row_out[m:m + 1, k * UNIT:(k + 1) * UNIT] = rn[i:i + 1]
    col_total = take(colsrc, colin, COL_SUMS, 16, in_row, at_row)
    for m in range(2):
        for j in range(TILES):
            i = m * TILES + j
            cn[i:i + 1] = decay_rate * colf[m:m + 1, j * LANES:(j + 1) * LANES] + (1.0 - decay_rate) * (
                col_total[i:i + 1] / FF + tiny_eps
            )
            col_out[m:m + 1, j * LANES:(j + 1) * LANES] = cn[i:i + 1]

    a[...] = 1.0 / rn[...]
    b[...] = 1.0 / cn[...]
    sumsrc[...] = jnp.zeros_like(sumsrc)
    for m in range(2):
        def norms(k, carry):
            rows = pl.ds(pl.multiple_of(k * UNIT, UNIT), UNIT)
            total = jnp.zeros((UNIT, LANES), F32)
            for j in range(TILES):
                v = g[m, rows, j * LANES:(j + 1) * LANES].astype(F32)
                total = total + v * v * b[m * TILES + j:m * TILES + j + 1]
            total = total * spread(a[pl.ds(m * PAIRS + k, 1), :])
            return carry + jnp.sum(total.reshape(UNIT // 8, 8, LANES), axis=0)

        parts = lax.fori_loop(0, PAIRS, norms, jnp.zeros((8, LANES), F32))
        sumsrc[0, m:m + 1] = jnp.sum(parts, axis=0, keepdims=True)
        sumsrc[0, 2 + m:3 + m] = jnp.sum(rn[m * PAIRS:(m + 1) * PAIRS], axis=0, keepdims=True)

    give(sumsrc.at[0], sum_xc, SUM_XC, 8, in_xc, at_xc)
    sumsrc[1] = take(sumsrc.at[0], sum_xc, SUM_XC, 8, in_xc, at_xc)
    give(sumsrc.at[1], sum_yz, SUM_YZ, 16, in_yz, at_yz)

    slots = [yh, 2, 1 - yh]
    for f in range(2):
        @pl.when(jnp.logical_not(same & (yh == f)))
        def _():
            remote(tok, t.at[f, mine], ty_s.at[f], ty_r.at[f], yh_peer).wait_recv()

    @pl.when(same)
    def _():
        other_send.wait_recv()

    def along_x(q, f, source):
        rows = rows_of(source, c)
        slot = slots[f]
        return remote(t.at[slot, rows], t.at[slot, rows], tx_s.at[q, f], tx_r.at[source, f], {"x": q})

    def to_sibling(q, f):
        rows = rows_of(q, c)
        slot = slots[f]
        return remote(t.at[slot, rows], t.at[slot, rows], tc_s.at[q, f], tc_r.at[q, f], sibling)

    def from_sibling(q, f):
        rows = rows_of(q, 1 - c)
        slot = slots[f]
        return remote(t.at[slot, rows], t.at[slot, rows], tc_s.at[q, f], tc_r.at[q, f], sibling)

    for f in range(3):
        for q in x_of:
            if f < 2 and q is not x_of[2]:
                @pl.when(same if f == 1 else jnp.logical_not(same))
                def _():
                    along_x(q, f, x).start()
            else:
                along_x(q, f, x).start()
        to_sibling(x, f).start()

    total = take(sumsrc.at[1], sum_yz, SUM_YZ, 16, in_yz, at_yz)

    for m in range(2):
        row_mean = jnp.sum(total[2 + m:3 + m], axis=1, keepdims=True) / (8.0 * FF)
        norm_total = jnp.sum(total[m:m + 1], axis=1, keepdims=True) * row_mean
        clip_scale = jnp.maximum(1.0, jnp.sqrt(norm_total / (FF * D)) / clip_limit)
        scale = learn_rate * jnp.sqrt(row_mean) / clip_scale
        a[m * PAIRS:(m + 1) * PAIRS] = scale / jnp.sqrt(rn[m * PAIRS:(m + 1) * PAIRS])
    b[...] = 1.0 / jnp.sqrt(cn[...])

    for copy in w_copies:
        copy.wait()

    def weight_send(k):
        return remote(wown.at[k], wpart.at[k], wy_s.at[k], wy_r.at[k], yh_peer)

    def update(i, carry):
        k = lax.rem(i + LOCAL // 2, PAIRS)
        rows = pl.ds(pl.multiple_of(k * UNIT, UNIT), UNIT)
        for m in range(2):
            factor = spread(a[pl.ds(m * PAIRS + k, 1), :])
            for j in range(TILES):
                cols = slice(j * LANES, (j + 1) * LANES)
                step = g[m, rows, cols].astype(F32) * factor * b[m * TILES + j:m * TILES + j + 1]
                new = (w[m, rows, cols].astype(F32) - step).astype(BF16)
                for h in range(2):
                    wown[2 * k + h, m * PIECE:(m + 1) * PIECE, cols] = new[h * PIECE:(h + 1) * PIECE]
        for h in range(2):
            @pl.when(2 * k + h >= LOCAL)
            def _():
                weight_send(2 * k + h).start()

        return carry

    lax.fori_loop(0, PAIRS, update, 0)

    def gather_tokens(f):
        for q in x_of:
            along_x(q, f, q).wait_recv()
            to_sibling(q, f).start()
        for q in [x] + x_of:
            from_sibling(q, f).wait_recv()

    gather_tokens(0)
    gather_tokens(1)

    right = lax.rem(z + 1, 4)
    left = lax.rem(z + 3, 4)

    def block_of(side, s):
        return lax.rem(z + 3 - s, 4) if side == 0 else lax.rem(z + 1 + s, 4)

    def ring_copy(n, s, side):
        target = right if side == 0 else left
        return remote(
            p.at[n, block_of(side, s), side], r.at[n, s, side],
            rs_s.at[n, s, side], rs_r.at[n, s, side], {"z": target},
        )

    def times(i, slot, weights):
        tokens = t[slot, pl.ds(pl.multiple_of(i * 2 * BLOCK, 2 * BLOCK), 2 * BLOCK), :]
        v = lax.dot_general(
            tokens, weights[...], (((1,), (1,)), ((), ())), preferred_element_type=F32
        )
        return v.reshape(2, 2, BLOCK // 2, LANES)

    def own_products(n):
        k = jnp.where(n < LOCAL, n, n - LOCAL)
        slot = jnp.where(n < LOCAL, 2, yh)

        def body(i, carry):
            p[n, pl.ds(2 * i, 2)] = times(i, slot, wown.at[k])
            return carry

        lax.fori_loop(0, 2, body, 0)

    def other_products(n):
        def body(i, carry):
            p[n, pl.ds(2 * i, 2)] += times(i, 1 - yh, wpart.at[n - LOCAL])
            return carry

        lax.fori_loop(0, 2, body, 0)

    def ring_step(n, s):
        for side in range(2):
            ring_copy(n, s - 1, side).wait_recv()
            p[n, block_of(side, s), side] += r[n, s - 1, side]
            ring_copy(n, s, side).start()

    def hidden(k, v):
        v = v.reshape(BLOCK, LANES)
        gate = v[:, :PIECE]
        up = v[:, PIECE:]
        h = (gate / (1.0 + jnp.exp(-gate)) * up).astype(BF16)

        @pl.when(lax.rem(k, 2) == 0)
        def _():
            hid[lax.div(k, 2), :, :PIECE] = h

        @pl.when(lax.rem(k, 2) == 1)
        def _():
            hid[lax.div(k, 2), :, PIECE:] = h

    def final_send(n):
        return remote(away.at[n], come.at[n], fy_s.at[n], fy_r.at[n], yh_peer)

    def finish(n):
        for side in range(2):
            ring_copy(n, 2, side).wait_recv()
        v = p[n, z] + r[n, 2]

        @pl.when(n < LOCAL)
        def _():
            away[n] = v
            final_send(n).start()

        @pl.when((n >= LOCAL) & (n < 2 * LOCAL))
        def _():
            kept[n - LOCAL] = v

        @pl.when(n >= 2 * LOCAL)
        def _():
            hidden(n - LOCAL, v)

    def work(n, carry):
        @pl.when(n < RINGS)
        def _():
            own_products(n)

        for s in (1, 2):
            @pl.when((n >= s * LAG) & (n < RINGS + s * LAG))
            def _():
                ring_step(n - s * LAG, s)

        @pl.when(n >= 3 * LAG)
        def _():
            finish(n - 3 * LAG)

        @pl.when(n == 2 * LOCAL)
        def _():
            gather_tokens(2)

        @pl.when((n >= 2 * LOCAL) & (n < RINGS))
        def _():
            weight_send(n - LOCAL).wait_recv()
            other_products(n)

        @pl.when(n < RINGS)
        def _():
            for side in range(2):
                ring_copy(n, 0, side).start()

        return carry

    lax.fori_loop(0, RINGS + 3 * LAG, work, 0)

    def last(n, carry):
        final_send(n).wait_recv()
        hidden(n, kept[n] + come[n])
        return carry

    lax.fori_loop(0, LOCAL, last, 0)

    for copy in sent:
        copy.wait_send()
    for q in range(2):
        @pl.when(jnp.logical_not(same & (yh == q)))
        def _():
            token_send(q).wait_send()

    @pl.when(jnp.logical_not(same))
    def _():
        other_send.wait_send()

    for f in range(3):
        for q in x_of:
            along_x(q, f, x).wait_send()
        for q in range(4):
            to_sibling(q, f).wait_send()

    def drain(n, carry):
        @pl.when(n >= 2 * LOCAL)
        def _():
            weight_send(n - LOCAL).wait_send()

        @pl.when(n < LOCAL)
        def _():
            final_send(n).wait_send()

        for s in range(3):
            for side in range(2):
                ring_copy(n, s, side).wait_send()
        return carry

    lax.fori_loop(0, RINGS, drain, 0)


def writer(hid, row_new, col_new, hid_out, row_out, col_out, sem):
    copies = [
        pltpu.make_async_copy(hid.at[k], hid_out.at[:, k * UNIT:(k + 1) * UNIT], sem.at[k])
        for k in range(PAIRS)
    ]
    copies += [
        pltpu.make_async_copy(row_new, row_out, sem.at[PAIRS]),
        pltpu.make_async_copy(col_new, col_out, sem.at[PAIRS + 1]),
    ]
    for copy in copies:
        copy.start()
    for copy in copies:
        copy.wait()


def local(tokens, weights, gradients, row_factors, col_factors):
    vmem = pl.BlockSpec(memory_space=pltpu.VMEM)
    hbm = pl.BlockSpec(memory_space=pl.ANY)
    dma = pltpu.SemaphoreType.DMA
    scratch = [
        pltpu.VMEM((2, ROWS, COLS), BF16),
        pltpu.VMEM((2, ROWS, COLS), BF16),
        pltpu.VMEM((CHUNKS, 2 * PIECE, COLS), BF16),
        pltpu.VMEM((CHUNKS, 2 * PIECE, COLS), BF16),
        pltpu.VMEM((3, HALF, COLS), BF16),
        pltpu.VMEM((RINGS, 4, 2, BLOCK // 2, LANES), F32),
        pltpu.VMEM((RINGS, 3, 2, BLOCK // 2, LANES), F32),
        pltpu.VMEM((LOCAL, 2, BLOCK // 2, LANES), F32),
        pltpu.VMEM((LOCAL, 2, BLOCK // 2, LANES), F32),
        pltpu.VMEM((LOCAL, 2, BLOCK // 2, LANES), F32),
        pltpu.VMEM((16, 8, LANES), F32),
        pltpu.VMEM((16, LANES), F32),
        pltpu.VMEM((16, LANES), F32),
        pltpu.VMEM((16, 16, LANES), F32),
        pltpu.VMEM((8, 16, LANES), F32),
        pltpu.VMEM((16, LANES), F32),
        pltpu.VMEM((16, LANES), F32),
        pltpu.VMEM((16, LANES), F32),
        pltpu.VMEM((16, LANES), F32),
        pltpu.VMEM((2, 8, LANES), F32),
        pltpu.VMEM((8, 8, LANES), F32),
        pltpu.VMEM((16, 8, LANES), F32),
        dma((2, PAIRS)), dma((2,)), dma((STAT_SEMS,)), dma((STAT_SEMS,)),
        dma((3,)), dma((3,)), dma((4, 3)), dma((4, 3)), dma((4, 3)), dma((4, 3)),
        dma((CHUNKS,)), dma((CHUNKS,)), dma((RINGS, 3, 2)), dma((RINGS, 3, 2)),
        dma((LOCAL,)), dma((LOCAL,)),
    ]
    results = pl.pallas_call(
        kernel,
        out_shape=[
            pltpu.VMEM((PAIRS, BLOCK, UNIT), BF16),
            pltpu.VMEM((2, ROWS), F32),
            pltpu.VMEM((2, COLS), F32),
        ],
        in_specs=[vmem, hbm, hbm, vmem, vmem],
        out_specs=[vmem, vmem, vmem],
        scratch_shapes=scratch,
        compiler_params=pltpu.CompilerParams(
            collective_id=0, has_side_effects=True, vmem_limit_bytes=52 * 2**20
        ),
        name="step",
    )(tokens, weights, gradients, row_factors, col_factors)
    return pl.pallas_call(
        writer,
        out_shape=[
            jax.ShapeDtypeStruct((BLOCK, ROWS), BF16),
            jax.ShapeDtypeStruct((2, ROWS), F32),
            jax.ShapeDtypeStruct((2, COLS), F32),
        ],
        in_specs=[vmem, vmem, vmem],
        out_specs=[hbm, hbm, hbm],
        scratch_shapes=[dma((PAIRS + 2,))],
        compiler_params=pltpu.CompilerParams(vmem_limit_bytes=2**20),
        name="write",
    )(*results)


def solution(mesh):
    torus = Mesh(mesh.devices.reshape(2, 4, 2, 2, 4), AXES)
    in_specs = (P(ROW, COL), P(None, ROW, COL), P(None, ROW, COL), P(None, ROW), P(None, COL))
    out_specs = (P(COL, ROW), P(None, ROW), P(None, COL))
    return jax.shard_map(local, mesh=torus, in_specs=in_specs, out_specs=out_specs, check_vma=False)
```

time: 133 us -> 124 us (0.932)
  Pallas kernels: 126 us -> 120 us
  local copies, waits for them, and re-layouts: 4.41 us -> 2.33 us
    pallas_call x1 -> x2, Pallas kernels: 126 us -> 120 us  [the longest x1 119 us: local(): pl.pallas_call(kernel, out_shape=[pltpu.VMEM((PAIRS, BLOCK, UNIT), BF16),...]
    unnamed x3 -> x6, local copies, waits for them, and re-layouts: 4.41 us -> 2.33 us
where the time goes in v2:
time: 124 us; the launch traced here: 123 us
  Pallas kernels  120 us (97%)
  local copies, waits for them, and re-layouts  2.33 us (2%)
    pallas_call x1, Pallas kernels, local(): pl.pallas_call(kernel, out_shape=[pltpu.VMEM((PAIRS, BLOCK, UNIT), BF16),...  119 us

profile of v2, /device:TPU:1, one launch (start us, length us, event | category | flops | bytes accessed | tf_op | source)
XLA Modules:
  0.0 123.1 jit_solution(13587034002203443595)
XLA Ops:
  0.6 0.0 copy-start
  0.6 0.9 copy-done
  1.6 0.0 copy-start.1
  1.6 0.7 copy-done.1
  2.3 0.0 copy-start.2
  2.3 0.7 copy-done.2
  3.0 119.3 %step.1 = (bf16[7,256,128]{2,1,0:T(8,128)(2,1)S(1)}, f32[2,896]{1,0:T(2,128)S(1)}, f32[2,1024]{1,0:T(2,128)S(1)}) custom-call(bf16[128,1024]{1,0:T(8,128)(2,1)S(1)} %copy-done, bf16[2,896,1024]{2,1,0:T(8,128)(2,1)} %wgt.1, bf16[2,896,1024]{2,1,0:T(8,128)(2,1)} %grd.1, f32[2,896]{1,0:T(2,128)S(1)} %copy-done.2, f32[2,1024]{1,0:T(2,128)S(1)} %copy-done.1), custom_call_target="tpu_custom_call" | custom-call | tf_op jit(solution)/shard_map/step/pallas_call | solution.py:491
  122.3 0.8 write.1
Async XLA Ops:
  0.6 1.0 copy-start
  1.6 0.7 copy-start.1
  2.3 0.7 copy-start.2

commit v3 on v2

--- a/solution.py
+++ b/solution.py
@@ -28,6 +28,7 @@
 CHUNKS = ROWS // PIECE
 LOCAL = 2
 RINGS = CHUNKS + LOCAL
+VMEM_LIMIT = 67043328 - 464 * 1024
 LAG = 2
 LANES = 128
 TILES = COLS // LANES
@@ -43,12 +44,12 @@
 
 
 def kernel(
-    tok, wgt, grd, rowf, colf,
+    tok, wgt, grd, row_old, col_old,
     hid, row_out, col_out,
-    g, w, wown, wpart, t, p, r, away, come, kept,
+    rowf, colf, g, w, wown, wpart, t, p, r, away, come, kept,
     colacc, colsrc, rowsrc, colin, rowin,
     rn, cn, a, b, sumsrc, sum_xc, sum_yz,
-    g_sem, w_sem, st_s, st_r, ty_s, ty_r, tx_s, tx_r, tc_s, tc_r,
+    g_sem, w_sem, in_sem, st_s, st_r, ty_s, ty_r, nx_s, nx_r, fx_s, fx_r, tc_s, tc_r,
     wy_s, wy_r, rs_s, rs_r, fy_s, fy_r,
 ):
     yl = lax.axis_index("yl")
@@ -74,7 +75,9 @@
     in_col = yh * 4 + z
     in_xc = x * 2 + c
     in_yz = y * 4 + z
-    x_of = [lax.rem(x + d, 4) for d in (1, 3, 2)]
+    x_next = lax.rem(x + 1, 4)
+    x_prev = lax.rem(x + 3, 4)
+    x_far = lax.rem(x + 2, 4)
     sibling = {"c": 1 - c}
     yh_peer = {"yh": 1 - yh}
 
@@ -92,7 +95,20 @@
         for k in range(PAIRS):
             g_copy(m, k).start()
     w_copies = [pltpu.make_async_copy(wgt.at[m], w.at[m], w_sem.at[m]) for m in range(2)]
-    for copy in w_copies:
+
+    def rows_of(q, core):
+        return pl.ds(pl.multiple_of((q * 2 + core) * 128, 128), 128)
+
+    mine = rows_of(x, c)
+    same = yl == yh
+    slots = [jnp.where(same, yh, 2), jnp.where(same, 2, yh), 1 - yh]
+    tok_copy = pltpu.make_async_copy(tok, t.at[slots[0], mine], in_sem.at[0])
+    tok_copy.start()
+    factor_copies = [
+        pltpu.make_async_copy(row_old, rowf, in_sem.at[1]),
+        pltpu.make_async_copy(col_old, colf, in_sem.at[2]),
+    ]
+    for copy in factor_copies + w_copies:
         copy.start()
 
     barrier = pltpu.get_barrier_semaphore()
@@ -144,32 +160,82 @@
     give(rowsrc, rowin, ROW_SUMS, 8, in_col, at_col)
     give(colsrc, colin, COL_SUMS, 16, in_row, at_row)
 
-    def rows_of(q, core):
-        return pl.ds(pl.multiple_of((q * 2 + core) * 128, 128), 128)
-
-    mine = rows_of(x, c)
-    same = yl == yh
-
-    def token_send(q):
-        return remote(tok, t.at[yh, mine], ty_s.at[q], ty_r.at[yh], {"yh": yl, "yl": q})
-
-    other_send = remote(tok, t.at[2, mine], ty_s.at[2], ty_r.at[2], {"yl": 1 - yl})
-    home = jnp.where(same, yh, 2)
-    t[home, mine] = tok[...]
-    early = [
-        remote(tok, t.at[home, mine], tx_s.at[q, jnp.where(same, 0, 1)], tx_r.at[x, jnp.where(same, 0, 1)], {"x": q})
-        for q in x_of[:2]
-    ]
-    for copy in early:
-        copy.start()
-    for q in range(2):
-        @pl.when(jnp.logical_not(same & (yh == q)))
-        def _():
-            token_send(q).start()
-
-    @pl.when(jnp.logical_not(same))
-    def _():
-        other_send.start()
+    def near(f, side):
+        rows = mine
+        return remote(
+            t.at[slots[f], rows], t.at[slots[f], rows], nx_s.at[f, side], nx_r.at[f, side],
+            {"x": x_next if side == 0 else x_prev},
+        )
+
+    def near_in(f, side):
+        rows = rows_of(x_prev if side == 0 else x_next, c)
+        return remote(
+            t.at[slots[f], rows], t.at[slots[f], rows], nx_s.at[f, side], nx_r.at[f, side],
+            {"x": x_next if side == 0 else x_prev},
+        )
+
+    def half_rows(q, side):
+        return pl.ds(pl.multiple_of((q * 2 + c) * 128 + 64 * side, 64), 64)
+
+    def onward(f, side):
+        rows = half_rows(x_prev if side == 0 else x_next, side)
+        return remote(
+            t.at[slots[f], rows], t.at[slots[f], rows], fx_s.at[f, side], fx_r.at[f, side],
+            {"x": x_next if side == 0 else x_prev},
+        )
+
+    def onward_in(f, side):
+        rows = half_rows(x_far, side)
+        return remote(
+            t.at[slots[f], rows], t.at[slots[f], rows], fx_s.at[f, side], fx_r.at[f, side],
+            {"x": x_next if side == 0 else x_prev},
+        )
+
+    def to_sibling(q, f):
+        rows = rows_of(q, c)
+        return remote(t.at[slots[f], rows], t.at[slots[f], rows], tc_s.at[q, f], tc_r.at[q, f], sibling)
+
+    def from_sibling(q, f):
+        rows = rows_of(q, 1 - c)
+        return remote(t.at[slots[f], rows], t.at[slots[f], rows], tc_s.at[q, f], tc_r.at[q, f], sibling)
+
+    pair_send = remote(t.at[slots[0], mine], t.at[slots[0], mine], ty_s.at[0], ty_r.at[0], {"yl": 1 - yl})
+    pair_in = remote(t.at[slots[1], mine], t.at[slots[1], mine], ty_s.at[0], ty_r.at[0], {"yl": 1 - yl})
+    across_send = remote(
+        t.at[slots[0], mine], t.at[yh, mine], ty_s.at[1], ty_r.at[1], {"yl": 1 - yl, "yh": 1 - yh}
+    )
+    across_in = remote(
+        t.at[slots[2], mine], t.at[slots[2], mine], ty_s.at[1], ty_r.at[1], {"yl": 1 - yl, "yh": 1 - yh}
+    )
+    far_send = remote(t.at[slots[0], mine], t.at[yh, mine], ty_s.at[2], ty_r.at[2], yh_peer)
+    far_in = remote(t.at[slots[2], mine], t.at[slots[2], mine], ty_s.at[2], ty_r.at[2], yh_peer)
+
+    def share(f):
+        for side in range(2):
+            near(f, side).start()
+        to_sibling(x, f).start()
+
+    def pass_on(f):
+        for side in range(2):
+            near_in(f, side).wait_recv()
+            onward(f, side).start()
+        to_sibling(x_prev, f).start()
+        to_sibling(x_next, f).start()
+
+    def complete(f):
+        for side in range(2):
+            onward_in(f, side).wait_recv()
+        to_sibling(x_far, f).start()
+
+    def complete_sibling(f):
+        for q in (x, x_prev, x_next, x_far):
+            from_sibling(q, f).wait_recv()
+
+    tok_copy.wait()
+    pair_send.start()
+    share(0)
+    for copy in factor_copies:
+        copy.wait()
 
     row_total = take(rowsrc, rowin, ROW_SUMS, 8, in_col, at_col)
     for m in range(2):
@@ -205,46 +271,19 @@
         sumsrc[0, m:m + 1] = jnp.sum(parts, axis=0, keepdims=True)
         sumsrc[0, 2 + m:3 + m] = jnp.sum(rn[m * PAIRS:(m + 1) * PAIRS], axis=0, keepdims=True)
 
-    give(sumsrc.at[0], sum_xc, SUM_XC, 8, in_xc, at_xc)
-    sumsrc[1] = take(sumsrc.at[0], sum_xc, SUM_XC, 8, in_xc, at_xc)
-    give(sumsrc.at[1], sum_yz, SUM_YZ, 16, in_yz, at_yz)
-
-    slots = [yh, 2, 1 - yh]
-    for f in range(2):
-        @pl.when(jnp.logical_not(same & (yh == f)))
-        def _():
-            remote(tok, t.at[f, mine], ty_s.at[f], ty_r.at[f], yh_peer).wait_recv()
-
-    @pl.when(same)
+    give(sumsrc.at[0], sum_yz, SUM_YZ, 16, in_yz, at_yz)
+
+    @pl.when(jnp.logical_not(same))
     def _():
-        other_send.wait_recv()
-
-    def along_x(q, f, source):
-        rows = rows_of(source, c)
-        slot = slots[f]
-        return remote(t.at[slot, rows], t.at[slot, rows], tx_s.at[q, f], tx_r.at[source, f], {"x": q})
-
-    def to_sibling(q, f):
-        rows = rows_of(q, c)
-        slot = slots[f]
-        return remote(t.at[slot, rows], t.at[slot, rows], tc_s.at[q, f], tc_r.at[q, f], sibling)
-
-    def from_sibling(q, f):
-        rows = rows_of(q, 1 - c)
-        slot = slots[f]
-        return remote(t.at[slot, rows], t.at[slot, rows], tc_s.at[q, f], tc_r.at[q, f], sibling)
-
-    for f in range(3):
-        for q in x_of:
-            if f < 2 and q is not x_of[2]:
-                @pl.when(same if f == 1 else jnp.logical_not(same))
-                def _():
-                    along_x(q, f, x).start()
-            else:
-                along_x(q, f, x).start()
-        to_sibling(x, f).start()
-
-    total = take(sumsrc.at[1], sum_yz, SUM_YZ, 16, in_yz, at_yz)
+        across_send.start()
+        far_send.start()
+
+    pass_on(0)
+    sumsrc[1] = take(sumsrc.at[0], sum_yz, SUM_YZ, 16, in_yz, at_yz)
+    give(sumsrc.at[1], sum_xc, SUM_XC, 8, in_xc, at_xc)
+    pair_in.wait_recv()
+    share(1)
+    total = take(sumsrc.at[1], sum_xc, SUM_XC, 8, in_xc, at_xc)
 
     for m in range(2):
         row_mean = jnp.sum(total[2 + m:3 + m], axis=1, keepdims=True) / (8.0 * FF)
@@ -278,17 +317,20 @@
 
         return carry
 
-    lax.fori_loop(0, PAIRS, update, 0)
-
-    def gather_tokens(f):
-        for q in x_of:
-            along_x(q, f, q).wait_recv()
-            to_sibling(q, f).start()
-        for q in [x] + x_of:
-            from_sibling(q, f).wait_recv()
-
-    gather_tokens(0)
-    gather_tokens(1)
+    lax.fori_loop(0, 3, update, 0)
+    complete(0)
+
+    @pl.when(jnp.logical_not(same))
+    def _():
+        across_in.wait_recv()
+        share(2)
+
+    lax.fori_loop(3, 5, update, 0)
+    pass_on(1)
+    lax.fori_loop(5, PAIRS, update, 0)
+    complete(1)
+    complete_sibling(0)
+    complete_sibling(1)
 
     right = lax.rem(z + 1, 4)
     left = lax.rem(z + 3, 4)
@@ -303,29 +345,26 @@
             rs_s.at[n, s, side], rs_r.at[n, s, side], {"z": target},
         )
 
-    def times(i, slot, weights):
-        tokens = t[slot, pl.ds(pl.multiple_of(i * 2 * BLOCK, 2 * BLOCK), 2 * BLOCK), :]
+    def times(block, slot, weights):
+        tokens = t[slot, pl.ds(pl.multiple_of(block * BLOCK, BLOCK), BLOCK), :]
         v = lax.dot_general(
             tokens, weights[...], (((1,), (1,)), ((), ())), preferred_element_type=F32
         )
-        return v.reshape(2, 2, BLOCK // 2, LANES)
+        return v.reshape(2, BLOCK // 2, LANES)
 
     def own_products(n):
         k = jnp.where(n < LOCAL, n, n - LOCAL)
         slot = jnp.where(n < LOCAL, 2, yh)
-
-        def body(i, carry):
-            p[n, pl.ds(2 * i, 2)] = times(i, slot, wown.at[k])
-            return carry
-
-        lax.fori_loop(0, 2, body, 0)
+        for d in (3, 1, 2, 0):
+            block = lax.rem(z + d, 4)
+            p[n, block] = times(block, slot, wown.at[k])
 
     def other_products(n):
-        def body(i, carry):
-            p[n, pl.ds(2 * i, 2)] += times(i, 1 - yh, wpart.at[n - LOCAL])
-            return carry
-
-        lax.fori_loop(0, 2, body, 0)
+        for d in (3, 1, 2, 0):
+            block = lax.rem(z + d, 4)
+            p[n, block] += times(block, 1 - yh, wpart.at[n - LOCAL])
+            if d in (3, 1):
+                ring_copy(n, 0, 0 if d == 3 else 1).start()
 
     def ring_step(n, s):
         for side in range(2):
@@ -382,19 +421,29 @@
         def _():
             finish(n - 3 * LAG)
 
+        @pl.when(n < 2 * LOCAL)
+        def _():
+            for side in range(2):
+                ring_copy(n, 0, side).start()
+
+        @pl.when(same & (n == 1))
+        def _():
+            far_in.wait_recv()
+            share(2)
+
+        @pl.when(n == 3)
+        def _():
+            pass_on(2)
+
         @pl.when(n == 2 * LOCAL)
         def _():
-            gather_tokens(2)
+            complete(2)
+            complete_sibling(2)
 
         @pl.when((n >= 2 * LOCAL) & (n < RINGS))
         def _():
             weight_send(n - LOCAL).wait_recv()
             other_products(n)
-
-        @pl.when(n < RINGS)
-        def _():
-            for side in range(2):
-                ring_copy(n, 0, side).start()
 
         return carry
 
@@ -409,18 +458,17 @@
 
     for copy in sent:
         copy.wait_send()
-    for q in range(2):
-        @pl.when(jnp.logical_not(same & (yh == q)))
-        def _():
-            token_send(q).wait_send()
+    pair_send.wait_send()
 
     @pl.when(jnp.logical_not(same))
     def _():
-        other_send.wait_send()
+        across_send.wait_send()
+        far_send.wait_send()
 
     for f in range(3):
-        for q in x_of:
-            along_x(q, f, x).wait_send()
+        for side in range(2):
+            near(f, side).wait_send()
+            onward(f, side).wait_send()
         for q in range(4):
             to_sibling(q, f).wait_send()
 
@@ -461,6 +509,8 @@
     hbm = pl.BlockSpec(memory_space=pl.ANY)
     dma = pltpu.SemaphoreType.DMA
     scratch = [
+        pltpu.VMEM((2, ROWS), F32),
+        pltpu.VMEM((2, COLS), F32),
         pltpu.VMEM((2, ROWS, COLS), BF16),
         pltpu.VMEM((2, ROWS, COLS), BF16),
         pltpu.VMEM((CHUNKS, 2 * PIECE, COLS), BF16),
@@ -483,8 +533,8 @@
         pltpu.VMEM((2, 8, LANES), F32),
         pltpu.VMEM((8, 8, LANES), F32),
         pltpu.VMEM((16, 8, LANES), F32),
-        dma((2, PAIRS)), dma((2,)), dma((STAT_SEMS,)), dma((STAT_SEMS,)),
-        dma((3,)), dma((3,)), dma((4, 3)), dma((4, 3)), dma((4, 3)), dma((4, 3)),
+        dma((2, PAIRS)), dma((2,)), dma((3,)), dma((STAT_SEMS,)), dma((STAT_SEMS,)),
+        dma((3,)), dma((3,)), dma((3, 2)), dma((3, 2)), dma((3, 2)), dma((3, 2)), dma((4, 3)), dma((4, 3)),
         dma((CHUNKS,)), dma((CHUNKS,)), dma((RINGS, 3, 2)), dma((RINGS, 3, 2)),
         dma((LOCAL,)), dma((LOCAL,)),
     ]
@@ -495,11 +545,11 @@
             pltpu.VMEM((2, ROWS), F32),
             pltpu.VMEM((2, COLS), F32),
         ],
-        in_specs=[vmem, hbm, hbm, vmem, vmem],
+        in_specs=[hbm] * 5,
         out_specs=[vmem, vmem, vmem],
         scratch_shapes=scratch,
         compiler_params=pltpu.CompilerParams(
-            collective_id=0, has_side_effects=True, vmem_limit_bytes=52 * 2**20
+            collective_id=0, has_side_effects=True, vmem_limit_bytes=VMEM_LIMIT
         ),
         name="step",
     )(tokens, weights, gradients, row_factors, col_factors)

time: 124 us -> 115 us (0.927); the launches traced: 123 us -> 113 us
  Pallas kernels: 120 us -> 112 us
  local copies, waits for them, and re-layouts: 2.33 us -> 0 us
    pallas_call x1, Pallas kernels: 119 us -> 111 us  [local(): pl.pallas_call(kernel, out_shape=[pltpu.VMEM((PAIRS, BLOCK, UNIT), BF16),...]
    unnamed x6 -> x0, local copies, waits for them, and re-layouts: 2.33 us -> none
where the time goes in v3:
time: 115 us; the launch traced here: 113 us
  Pallas kernels  112 us (97%)
    pallas_call x1, Pallas kernels, local(): pl.pallas_call(kernel, out_shape=[pltpu.VMEM((PAIRS, BLOCK, UNIT), BF16),...  111 us

profile of v3, /device:TPU:1, one launch (start us, length us, event | category | flops | bytes accessed | tf_op | source)
XLA Modules:
  0.0 112.8 jit_solution(17052172921107792794)
XLA Ops:
  0.6 111.3 %step.1 = (bf16[7,256,128]{2,1,0:T(8,128)(2,1)S(1)}, f32[2,896]{1,0:T(2,128)S(1)}, f32[2,1024]{1,0:T(2,128)S(1)}) custom-call(bf16[128,1024]{1,0:T(8,128)(2,1)} %tok.1, bf16[2,896,1024]{2,1,0:T(8,128)(2,1)} %wgt.1, bf16[2,896,1024]{2,1,0:T(8,128)(2,1)} %grd.1, f32[2,896]{1,0:T(2,128)} %row_old.1, f32[2,1024]{1,0:T(2,128)} %col_old.1), custom_call_target="tpu_custom_call" | custom-call | tf_op jit(solution)/shard_map/step/pallas_call | solution.py:541
  112.0 0.8 write.1

commit v4 on v3

--- a/solution.py
+++ b/solution.py
@@ -24,12 +24,17 @@
 COLS = 1024
 UNIT = 128
 PAIRS = ROWS // UNIT
-PIECE = 64
-CHUNKS = ROWS // PIECE
-LOCAL = 2
+CHUNKS = PAIRS
+LOCAL = 4
 RINGS = CHUNKS + LOCAL
 VMEM_LIMIT = 67043328 - 464 * 1024
 LAG = 2
+WIDE = 2 * UNIT
+VALUES = WIDE
+MESSAGE = VALUES + 16
+SPAN = 250.0
+HALF_LOG = 125.0 * 0.6931471805599453
+ORDER = [LOCAL, 0, LOCAL + 1] + list(range(1, LOCAL)) + list(range(LOCAL + 2, CHUNKS))
 LANES = 128
 TILES = COLS // LANES
 HALF = 1024
@@ -43,10 +48,26 @@
     return jnp.transpose(jnp.broadcast_to(row, (LANES, LANES)))
 
 
+def put_code(ref, v):
+    v = v.reshape(-1, 8, LANES)
+    top = jnp.maximum(jnp.max(jnp.abs(v), axis=0) * 1.004, 1e-30).astype(BF16)
+    factor = SPAN / top.astype(F32)
+    q = jnp.exp2(jnp.abs(v) * factor - SPAN / 2.0)
+    ref[:VALUES] = jnp.where(v < 0.0, -q, q).reshape(VALUES, LANES).astype(BF16)
+    ref[VALUES:] = jnp.concatenate([top, top], axis=0)
+
+
+def get_code(ref):
+    top = ref[VALUES:].astype(F32)[:8]
+    q = ref[:VALUES].astype(F32).reshape(-1, 8, LANES)
+    v = (jnp.log(jnp.abs(q)) + HALF_LOG) * (top * (1.0 / (2.0 * HALF_LOG)))
+    return jnp.where(q < 0.0, -v, v).reshape(VALUES, LANES)
+
+
 def kernel(
     tok, wgt, grd, row_old, col_old,
     hid, row_out, col_out,
-    rowf, colf, g, w, wown, wpart, t, p, r, away, come, kept,
+    rowf, colf, g, w, wown, wpart, t, p, e, r, away, come, kept,
     colacc, colsrc, rowsrc, colin, rowin,
     rn, cn, a, b, sumsrc, sum_xc, sum_yz,
     g_sem, w_sem, in_sem, st_s, st_r, ty_s, ty_r, nx_s, nx_r, fx_s, fx_r, tc_s, tc_r,
@@ -148,10 +169,13 @@
             sent.append(copy)
         slots[me] = src[...]
 
-    def take(src, slots, place, n, me, device_of):
+    def arrive(src, slots, place, n, me, device_of):
         for d in range(1, n):
             q = lax.rem(me + d, n)
             remote(src, slots.at[q], st_s.at[place + q], st_r.at[place + q], device_of(q)).wait_recv()
+
+    def take(src, slots, place, n, me, device_of):
+        arrive(src, slots, place, n, me, device_of)
         total = slots[0]
         for q in range(1, n):
             total = total + slots[q]
@@ -233,9 +257,19 @@
 
     tok_copy.wait()
     pair_send.start()
+
+    @pl.when(jnp.logical_not(same))
+    def _():
+        across_send.start()
+        far_send.start()
+
     share(0)
     for copy in factor_copies:
         copy.wait()
+
+    for copy in w_copies:
+        copy.wait()
+    sumsrc[...] = jnp.zeros_like(sumsrc)
 
     row_total = take(rowsrc, rowin, ROW_SUMS, 8, in_col, at_col)
     for m in range(2):
@@ -256,7 +290,6 @@
 
     a[...] = 1.0 / rn[...]
     b[...] = 1.0 / cn[...]
-    sumsrc[...] = jnp.zeros_like(sumsrc)
     for m in range(2):
         def norms(k, carry):
             rows = pl.ds(pl.multiple_of(k * UNIT, UNIT), UNIT)
@@ -271,19 +304,13 @@
         sumsrc[0, m:m + 1] = jnp.sum(parts, axis=0, keepdims=True)
         sumsrc[0, 2 + m:3 + m] = jnp.sum(rn[m * PAIRS:(m + 1) * PAIRS], axis=0, keepdims=True)
 
-    give(sumsrc.at[0], sum_yz, SUM_YZ, 16, in_yz, at_yz)
-
-    @pl.when(jnp.logical_not(same))
-    def _():
-        across_send.start()
-        far_send.start()
-
-    pass_on(0)
-    sumsrc[1] = take(sumsrc.at[0], sum_yz, SUM_YZ, 16, in_yz, at_yz)
-    give(sumsrc.at[1], sum_xc, SUM_XC, 8, in_xc, at_xc)
+    give(sumsrc.at[0], sum_xc, SUM_XC, 8, in_xc, at_xc)
     pair_in.wait_recv()
     share(1)
-    total = take(sumsrc.at[1], sum_xc, SUM_XC, 8, in_xc, at_xc)
+    pass_on(0)
+    sumsrc[1] = take(sumsrc.at[0], sum_xc, SUM_XC, 8, in_xc, at_xc)
+    give(sumsrc.at[1], sum_yz, SUM_YZ, 16, in_yz, at_yz)
+    total = take(sumsrc.at[1], sum_yz, SUM_YZ, 16, in_yz, at_yz)
 
     for m in range(2):
         row_mean = jnp.sum(total[2 + m:3 + m], axis=1, keepdims=True) / (8.0 * FF)
@@ -293,41 +320,41 @@
         a[m * PAIRS:(m + 1) * PAIRS] = scale / jnp.sqrt(rn[m * PAIRS:(m + 1) * PAIRS])
     b[...] = 1.0 / jnp.sqrt(cn[...])
 
-    for copy in w_copies:
-        copy.wait()
-
     def weight_send(k):
-        return remote(wown.at[k], wpart.at[k], wy_s.at[k], wy_r.at[k], yh_peer)
+        return remote(wown.at[k], wpart.at[k - LOCAL], wy_s.at[k], wy_r.at[k], yh_peer)
 
     def update(i, carry):
-        k = lax.rem(i + LOCAL // 2, PAIRS)
+        k = ORDER[-1]
+        for q in range(CHUNKS - 1):
+            k = jnp.where(i == q, ORDER[q], k)
         rows = pl.ds(pl.multiple_of(k * UNIT, UNIT), UNIT)
         for m in range(2):
             factor = spread(a[pl.ds(m * PAIRS + k, 1), :])
             for j in range(TILES):
                 cols = slice(j * LANES, (j + 1) * LANES)
                 step = g[m, rows, cols].astype(F32) * factor * b[m * TILES + j:m * TILES + j + 1]
-                new = (w[m, rows, cols].astype(F32) - step).astype(BF16)
-                for h in range(2):
-                    wown[2 * k + h, m * PIECE:(m + 1) * PIECE, cols] = new[h * PIECE:(h + 1) * PIECE]
-        for h in range(2):
-            @pl.when(2 * k + h >= LOCAL)
-            def _():
-                weight_send(2 * k + h).start()
+                wown[k, m * UNIT:(m + 1) * UNIT, cols] = (w[m, rows, cols].astype(F32) - step).astype(BF16)
+
+        @pl.when(k >= LOCAL)
+        def _():
+            weight_send(k).start()
 
         return carry
 
-    lax.fori_loop(0, 3, update, 0)
-    complete(0)
+    lax.fori_loop(0, 1, update, 0)
+    pass_on(1)
+
+    @pl.when(same)
+    def _():
+        far_in.wait_recv()
 
     @pl.when(jnp.logical_not(same))
     def _():
         across_in.wait_recv()
-        share(2)
-
-    lax.fori_loop(3, 5, update, 0)
-    pass_on(1)
-    lax.fori_loop(5, PAIRS, update, 0)
+
+    share(2)
+    lax.fori_loop(1, 3, update, 0)
+    complete(0)
     complete(1)
     complete_sibling(0)
     complete_sibling(1)
@@ -341,50 +368,66 @@
     def ring_copy(n, s, side):
         target = right if side == 0 else left
         return remote(
-            p.at[n, block_of(side, s), side], r.at[n, s, side],
+            e.at[n, s, side], r.at[n, s, side],
             rs_s.at[n, s, side], rs_r.at[n, s, side], {"z": target},
         )
 
     def times(block, slot, weights):
         tokens = t[slot, pl.ds(pl.multiple_of(block * BLOCK, BLOCK), BLOCK), :]
-        v = lax.dot_general(
+        return lax.dot_general(
             tokens, weights[...], (((1,), (1,)), ((), ())), preferred_element_type=F32
         )
-        return v.reshape(2, BLOCK // 2, LANES)
-
-    def own_products(n):
+
+    def arrange(v):
+        parts = []
+        for side in range(2):
+            rows = slice(side * (BLOCK // 2), (side + 1) * (BLOCK // 2))
+            parts.append(jnp.concatenate([v[rows, :UNIT], v[rows, UNIT:]], axis=0))
+        return parts
+
+    def begin(n, d, parts):
+        if d in (3, 1):
+            side = 0 if d == 3 else 1
+            put_code(e.at[n, 0, side], parts[side])
+            ring_copy(n, 0, side).start()
+
+    def local_products(n):
         k = jnp.where(n < LOCAL, n, n - LOCAL)
         slot = jnp.where(n < LOCAL, 2, yh)
         for d in (3, 1, 2, 0):
             block = lax.rem(z + d, 4)
-            p[n, block] = times(block, slot, wown.at[k])
+            parts = arrange(times(block, slot, wown.at[k]))
+            for side in range(2):
+                p[n, block, side] = parts[side]
+            begin(n, d, parts)
+
+    def own_products(n):
+        for d in (3, 1, 2, 0):
+            block = lax.rem(z + d, 4)
+            parts = arrange(times(block, yh, wown.at[n - LOCAL]))
+            for side in range(2):
+                p[n, block, side] = parts[side]
 
     def other_products(n):
         for d in (3, 1, 2, 0):
             block = lax.rem(z + d, 4)
-            p[n, block] += times(block, 1 - yh, wpart.at[n - LOCAL])
-            if d in (3, 1):
-                ring_copy(n, 0, 0 if d == 3 else 1).start()
+            parts = arrange(times(block, 1 - yh, wpart.at[n - 2 * LOCAL]))
+            for side in range(2):
+                parts[side] = parts[side] + p[n, block, side]
+                p[n, block, side] = parts[side]
+            begin(n, d, parts)
 
     def ring_step(n, s):
         for side in range(2):
             ring_copy(n, s - 1, side).wait_recv()
-            p[n, block_of(side, s), side] += r[n, s - 1, side]
+            put_code(e.at[n, s, side], p[n, block_of(side, s), side] + get_code(r.at[n, s - 1, side]))
             ring_copy(n, s, side).start()
 
-    def hidden(k, v):
-        v = v.reshape(BLOCK, LANES)
-        gate = v[:, :PIECE]
-        up = v[:, PIECE:]
-        h = (gate / (1.0 + jnp.exp(-gate)) * up).astype(BF16)
-
-        @pl.when(lax.rem(k, 2) == 0)
-        def _():
-            hid[lax.div(k, 2), :, :PIECE] = h
-
-        @pl.when(lax.rem(k, 2) == 1)
-        def _():
-            hid[lax.div(k, 2), :, PIECE:] = h
+    def hidden(k, side, v):
+        gate = v[:UNIT]
+        up = v[UNIT:]
+        rows = slice(side * (BLOCK // 2), (side + 1) * (BLOCK // 2))
+        hid[k, rows] = (gate / (1.0 + jnp.exp(-gate)) * up).astype(BF16)
 
     def final_send(n):
         return remote(away.at[n], come.at[n], fy_s.at[n], fy_r.at[n], yh_peer)
@@ -392,25 +435,36 @@
     def finish(n):
         for side in range(2):
             ring_copy(n, 2, side).wait_recv()
-        v = p[n, z] + r[n, 2]
+            v = p[n, z, side] + get_code(r.at[n, 2, side])
+
+            @pl.when(n < LOCAL)
+            def _():
+                put_code(away.at[n, side], v)
+
+            @pl.when((n >= LOCAL) & (n < 2 * LOCAL))
+            def _():
+                kept[n - LOCAL, side] = v
+
+            @pl.when(n >= 2 * LOCAL)
+            def _():
+                hidden(n - LOCAL, side, v)
 
         @pl.when(n < LOCAL)
         def _():
-            away[n] = v
             final_send(n).start()
 
-        @pl.when((n >= LOCAL) & (n < 2 * LOCAL))
-        def _():
-            kept[n - LOCAL] = v
-
-        @pl.when(n >= 2 * LOCAL)
-        def _():
-            hidden(n - LOCAL, v)
-
     def work(n, carry):
-        @pl.when(n < RINGS)
+        @pl.when(n < 2 * LOCAL)
+        def _():
+            local_products(n)
+
+        @pl.when((n >= 2 * LOCAL) & (n < RINGS))
         def _():
             own_products(n)
+
+        @pl.when(n < PAIRS - 3)
+        def _():
+            update(n + 3, 0)
 
         for s in (1, 2):
             @pl.when((n >= s * LAG) & (n < RINGS + s * LAG))
@@ -421,17 +475,7 @@
         def _():
             finish(n - 3 * LAG)
 
-        @pl.when(n < 2 * LOCAL)
-        def _():
-            for side in range(2):
-                ring_copy(n, 0, side).start()
-
-        @pl.when(same & (n == 1))
-        def _():
-            far_in.wait_recv()
-            share(2)
-
-        @pl.when(n == 3)
+        @pl.when(n == 2)
         def _():
             pass_on(2)
 
@@ -451,7 +495,8 @@
 
     def last(n, carry):
         final_send(n).wait_recv()
-        hidden(n, kept[n] + come[n])
+        for side in range(2):
+            hidden(n, side, kept[n, side] + get_code(come.at[n, side]))
         return carry
 
     lax.fori_loop(0, LOCAL, last, 0)
@@ -513,14 +558,15 @@
         pltpu.VMEM((2, COLS), F32),
         pltpu.VMEM((2, ROWS, COLS), BF16),
         pltpu.VMEM((2, ROWS, COLS), BF16),
-        pltpu.VMEM((CHUNKS, 2 * PIECE, COLS), BF16),
-        pltpu.VMEM((CHUNKS, 2 * PIECE, COLS), BF16),
+        pltpu.VMEM((CHUNKS, WIDE, COLS), BF16),
+        pltpu.VMEM((CHUNKS - LOCAL, WIDE, COLS), BF16),
         pltpu.VMEM((3, HALF, COLS), BF16),
-        pltpu.VMEM((RINGS, 4, 2, BLOCK // 2, LANES), F32),
-        pltpu.VMEM((RINGS, 3, 2, BLOCK // 2, LANES), F32),
-        pltpu.VMEM((LOCAL, 2, BLOCK // 2, LANES), F32),
-        pltpu.VMEM((LOCAL, 2, BLOCK // 2, LANES), F32),
-        pltpu.VMEM((LOCAL, 2, BLOCK // 2, LANES), F32),
+        pltpu.VMEM((RINGS, 4, 2, VALUES, LANES), F32),
+        pltpu.VMEM((RINGS, 3, 2, MESSAGE, LANES), BF16),
+        pltpu.VMEM((RINGS, 3, 2, MESSAGE, LANES), BF16),
+        pltpu.VMEM((LOCAL, 2, MESSAGE, LANES), BF16),
+        pltpu.VMEM((LOCAL, 2, MESSAGE, LANES), BF16),
+        pltpu.VMEM((LOCAL, 2, VALUES, LANES), F32),
         pltpu.VMEM((16, 8, LANES), F32),
         pltpu.VMEM((16, LANES), F32),
         pltpu.VMEM((16, LANES), F32),

time: 115 us -> 91.9 us (0.80); the launches traced: 113 us -> 91.8 us
  Pallas kernels: 112 us -> 91.2 us
    pallas_call x1, Pallas kernels: 111 us -> 90.3 us  [local(): pl.pallas_call(kernel, out_shape=[pltpu.VMEM((PAIRS, BLOCK, UNIT), BF16),...]
where the time goes in v4:
time: 91.9 us; the launch traced here: 91.8 us
  Pallas kernels  91.2 us (99%)
    pallas_call x1, Pallas kernels, local(): pl.pallas_call(kernel, out_shape=[pltpu.VMEM((PAIRS, BLOCK, UNIT), BF16),...  90.3 us

profile of v4, /device:TPU:1, one launch (start us, length us, event | category | flops | bytes accessed | tf_op | source)
XLA Modules:
  0.0 91.8 jit_solution(12597164210094390263)
XLA Ops:
  0.6 90.3 %step.1 = (bf16[7,256,128]{2,1,0:T(8,128)(2,1)S(1)}, f32[2,896]{1,0:T(2,128)S(1)}, f32[2,1024]{1,0:T(2,128)S(1)}) custom-call(bf16[128,1024]{1,0:T(8,128)(2,1)} %tok.1, bf16[2,896,1024]{2,1,0:T(8,128)(2,1)} %wgt.1, bf16[2,896,1024]{2,1,0:T(8,128)(2,1)} %grd.1, f32[2,896]{1,0:T(2,128)} %row_old.1, f32[2,1024]{1,0:T(2,128)} %col_old.1), custom_call_target="tpu_custom_call" | custom-call | tf_op jit(solution)/shard_map/step/pallas_call | solution.py:587
  91.0 0.8 write.1

commit v5 on v4

--- a/solution.py
+++ b/solution.py
@@ -34,7 +34,7 @@
 MESSAGE = VALUES + 16
 SPAN = 250.0
 HALF_LOG = 125.0 * 0.6931471805599453
-ORDER = [LOCAL, 0, LOCAL + 1] + list(range(1, LOCAL)) + list(range(LOCAL + 2, CHUNKS))
+ORDER = [0, LOCAL, 1, LOCAL + 1] + list(range(2, LOCAL)) + list(range(LOCAL + 2, CHUNKS))
 LANES = 128
 TILES = COLS // LANES
 HALF = 1024
@@ -305,11 +305,12 @@
         sumsrc[0, 2 + m:3 + m] = jnp.sum(rn[m * PAIRS:(m + 1) * PAIRS], axis=0, keepdims=True)
 
     give(sumsrc.at[0], sum_xc, SUM_XC, 8, in_xc, at_xc)
+    pass_on(0)
     pair_in.wait_recv()
     share(1)
-    pass_on(0)
     sumsrc[1] = take(sumsrc.at[0], sum_xc, SUM_XC, 8, in_xc, at_xc)
     give(sumsrc.at[1], sum_yz, SUM_YZ, 16, in_yz, at_yz)
+    complete(0)
     total = take(sumsrc.at[1], sum_yz, SUM_YZ, 16, in_yz, at_yz)
 
     for m in range(2):
@@ -341,23 +342,8 @@
 
         return carry
 
-    lax.fori_loop(0, 1, update, 0)
-    pass_on(1)
-
-    @pl.when(same)
-    def _():
-        far_in.wait_recv()
-
-    @pl.when(jnp.logical_not(same))
-    def _():
-        across_in.wait_recv()
-
-    share(2)
-    lax.fori_loop(1, 3, update, 0)
-    complete(0)
-    complete(1)
+    lax.fori_loop(0, 2, update, 0)
     complete_sibling(0)
-    complete_sibling(1)
 
     right = lax.rem(z + 1, 4)
     left = lax.rem(z + 3, 4)
@@ -393,7 +379,7 @@
 
     def local_products(n):
         k = jnp.where(n < LOCAL, n, n - LOCAL)
-        slot = jnp.where(n < LOCAL, 2, yh)
+        slot = jnp.where(n < LOCAL, slots[0], slots[1])
         for d in (3, 1, 2, 0):
             block = lax.rem(z + d, 4)
             parts = arrange(times(block, slot, wown.at[k]))
@@ -432,26 +418,29 @@
     def final_send(n):
         return remote(away.at[n], come.at[n], fy_s.at[n], fy_r.at[n], yh_peer)
 
+    def leaves(n):
+        return (jnp.logical_not(same) & (n < LOCAL)) | (same & (n >= LOCAL) & (n < 2 * LOCAL))
+
     def finish(n):
         for side in range(2):
             ring_copy(n, 2, side).wait_recv()
             v = p[n, z, side] + get_code(r.at[n, 2, side])
 
-            @pl.when(n < LOCAL)
+            @pl.when(leaves(n))
             def _():
-                put_code(away.at[n, side], v)
-
-            @pl.when((n >= LOCAL) & (n < 2 * LOCAL))
+                put_code(away.at[lax.rem(n, LOCAL), side], v)
+
+            @pl.when(jnp.logical_not(leaves(n)) & (n < 2 * LOCAL))
             def _():
-                kept[n - LOCAL, side] = v
+                kept[lax.rem(n, LOCAL), side] = v
 
             @pl.when(n >= 2 * LOCAL)
             def _():
                 hidden(n - LOCAL, side, v)
 
-        @pl.when(n < LOCAL)
-        def _():
-            final_send(n).start()
+        @pl.when(leaves(n))
+        def _():
+            final_send(lax.rem(n, LOCAL)).start()
 
     def work(n, carry):
         @pl.when(n < 2 * LOCAL)
@@ -464,7 +453,7 @@
 
         @pl.when(n < PAIRS - 3)
         def _():
-            update(n + 3, 0)
+            lax.fori_loop(jnp.where(n == 0, 2, n + 3), n + 4, update, 0)
 
         for s in (1, 2):
             @pl.when((n >= s * LAG) & (n < RINGS + s * LAG))
@@ -475,9 +464,30 @@
         def _():
             finish(n - 3 * LAG)
 
+        @pl.when(n == 1)
+        def _():
+            pass_on(1)
+
         @pl.when(n == 2)
         def _():
+            @pl.when(same)
+            def _():
+                far_in.wait_recv()
+
+            @pl.when(jnp.logical_not(same))
+            def _():
+                across_in.wait_recv()
+
+            share(2)
+
+        @pl.when(n == LOCAL + 1)
+        def _():
             pass_on(2)
+
+        @pl.when(n == LOCAL - 1)
+        def _():
+            complete(1)
+            complete_sibling(1)
 
         @pl.when(n == 2 * LOCAL)
         def _():

time: 91.9 us -> 86.4 us (0.940)
  Pallas kernels: 91.2 us -> 85.6 us
    pallas_call x1, Pallas kernels: 90.3 us -> 84.8 us  [local(): pl.pallas_call(kernel, out_shape=[pltpu.VMEM((PAIRS, BLOCK, UNIT), BF16),...]
where the time goes in v5:
time: 86.4 us; the launch traced here: 86.3 us
  Pallas kernels  85.6 us (99%)
    pallas_call x1, Pallas kernels, local(): pl.pallas_call(kernel, out_shape=[pltpu.VMEM((PAIRS, BLOCK, UNIT), BF16),...  84.8 us

profile of v5, /device:TPU:1, one launch (start us, length us, event | category | flops | bytes accessed | tf_op | source)
XLA Modules:
  0.0 86.3 jit_solution(5844469040594134791)
XLA Ops:
  0.6 84.8 %step.1 = (bf16[7,256,128]{2,1,0:T(8,128)(2,1)S(1)}, f32[2,896]{1,0:T(2,128)S(1)}, f32[2,1024]{1,0:T(2,128)S(1)}) custom-call(bf16[128,1024]{1,0:T(8,128)(2,1)} %tok.1, bf16[2,896,1024]{2,1,0:T(8,128)(2,1)} %wgt.1, bf16[2,896,1024]{2,1,0:T(8,128)(2,1)} %grd.1, f32[2,896]{1,0:T(2,128)} %row_old.1, f32[2,1024]{1,0:T(2,128)} %col_old.1), custom_call_target="tpu_custom_call" | custom-call | tf_op jit(solution)/shard_map/step/pallas_call | solution.py:597
  85.4 0.8 write.1

commit v6 on v5

--- a/solution.py
+++ b/solution.py
@@ -464,11 +464,11 @@
         def _():
             finish(n - 3 * LAG)
 
-        @pl.when(n == 1)
+        @pl.when(n == 0)
         def _():
             pass_on(1)
 
-        @pl.when(n == 2)
+        @pl.when(n == 4)
         def _():
             @pl.when(same)
             def _():
@@ -480,7 +480,7 @@
 
             share(2)
 
-        @pl.when(n == LOCAL + 1)
+        @pl.when(n == LOCAL + 2)
         def _():
             pass_on(2)
 

time: 86.4 us -> 85.6 us (level)
  no operation moved by 1% of the time
where the time goes in v6:
time: 85.6 us; the launch traced here: 85.5 us
  Pallas kernels  84.8 us (99%)
    pallas_call x1, Pallas kernels, local(): pl.pallas_call(kernel, out_shape=[pltpu.VMEM((PAIRS, BLOCK, UNIT), BF16),...  84 us

profile of v6, /device:TPU:1, one launch (start us, length us, event | category | flops | bytes accessed | tf_op | source)
XLA Modules:
  0.0 85.5 jit_solution(1356085107782733574)
XLA Ops:
  0.6 84.0 %step.1 = (bf16[7,256,128]{2,1,0:T(8,128)(2,1)S(1)}, f32[2,896]{1,0:T(2,128)S(1)}, f32[2,1024]{1,0:T(2,128)S(1)}) custom-call(bf16[128,1024]{1,0:T(8,128)(2,1)} %tok.1, bf16[2,896,1024]{2,1,0:T(8,128)(2,1)} %wgt.1, bf16[2,896,1024]{2,1,0:T(8,128)(2,1)} %grd.1, f32[2,896]{1,0:T(2,128)} %row_old.1, f32[2,1024]{1,0:T(2,128)} %col_old.1), custom_call_target="tpu_custom_call" | custom-call | tf_op jit(solution)/shard_map/step/pallas_call | solution.py:597
  84.6 0.8 write.1

commit v7 on v6

--- a/solution.py
+++ b/solution.py
@@ -342,7 +342,7 @@
 
         return carry
 
-    lax.fori_loop(0, 2, update, 0)
+    lax.fori_loop(0, 1, update, 0)
     complete_sibling(0)
 
     right = lax.rem(z + 1, 4)
@@ -453,7 +453,7 @@
 
         @pl.when(n < PAIRS - 3)
         def _():
-            lax.fori_loop(jnp.where(n == 0, 2, n + 3), n + 4, update, 0)
+            lax.fori_loop(jnp.where(n == 0, 1, n + 3), n + 4, update, 0)
 
         for s in (1, 2):
             @pl.when((n >= s * LAG) & (n < RINGS + s * LAG))

time: 85.6 us -> 85.6 us (level)
  no operation moved by 1% of the time
where the time goes in v7:
time: 85.6 us; the launch traced here: 85.5 us
  Pallas kernels  84.9 us (99%)
    pallas_call x1, Pallas kernels, local(): pl.pallas_call(kernel, out_shape=[pltpu.VMEM((PAIRS, BLOCK, UNIT), BF16),...  84 us

profile of v7, /device:TPU:1, one launch (start us, length us, event | category | flops | bytes accessed | tf_op | source)
XLA Modules:
  0.0 85.5 jit_solution(14793572785363160837)
XLA Ops:
  0.6 84.0 %step.1 = (bf16[7,256,128]{2,1,0:T(8,128)(2,1)S(1)}, f32[2,896]{1,0:T(2,128)S(1)}, f32[2,1024]{1,0:T(2,128)S(1)}) custom-call(bf16[128,1024]{1,0:T(8,128)(2,1)} %tok.1, bf16[2,896,1024]{2,1,0:T(8,128)(2,1)} %wgt.1, bf16[2,896,1024]{2,1,0:T(8,128)(2,1)} %grd.1, f32[2,896]{1,0:T(2,128)} %row_old.1, f32[2,1024]{1,0:T(2,128)} %col_old.1), custom_call_target="tpu_custom_call" | custom-call | tf_op jit(solution)/shard_map/step/pallas_call | solution.py:597
  84.6 0.8 write.1
